TPU v7x, 32 devices: a whole 2x2x4 slice. The times are simulated.
32 devices in a mesh: brick: 16 (over z, y, core), chan: 2 (over x).
Axes of the slice: x: 2, y: 2, z: 4, core: 2. Of those that a mesh axis runs over, the one named last changes fastest.
Arguments:
- volume: bfloat16 [32, 16, 64, 256], P('brick', 'chan'), may hold values from -6 to 6
- first_weight: bfloat16 [3, 3, 3, 256, 256], replicated, may hold values from -0.078125 to 0.078125
- second_weight: bfloat16 [3, 3, 3, 256, 256], replicated, may hold values from -0.078125 to 0.078125
- coarse_weight: bfloat16 [3, 3, 3, 256, 512], P(None, None, None, None, 'chan'), may hold values from -0.078125 to 0.078125
- projection: bfloat16 [512, 256], P('chan'), may hold values from -0.25 to 0.25
Outputs:
- merged: bfloat16 [32, 16, 64, 256], P('brick', 'chan')
All inputs are finite; a program needn't handle non-finite values.
Results may differ from a plain program's by a relative error of at most 0.011.
Values may be sent and summed in bfloat16 or wider, within the bound.
No kernel may reach another device: no remote copies, remote signals or barrier semaphores. Data moves between devices by JAX's collectives and lax.ppermute only.
A program may use at most 64 MiB of HBM per device.

v0:
```python
import functools

import jax
import jax.numpy as jnp
from jax import lax
from jax.experimental import pallas as pl
from jax.experimental.pallas import tpu as pltpu
from jax.sharding import PartitionSpec as P


AXES = ("brick", "chan")
BF16 = jnp.bfloat16
F32 = jnp.float32
LANES = 128
WEIGHT_COPY_FLOPS = 2**33
VMEM_SPEC = pl.BlockSpec(memory_space=pltpu.VMEM)


def brick_partner(kind, brick, bricks):
    if kind == "own":
        return brick
    partner = brick ^ 1 if kind == "near" else ((brick + 1) ^ 1) - 1
    return partner if 0 <= partner < bricks else None


def exchange(value, kind, chan_of=None):
    bricks, chans = lax.axis_size("brick"), lax.axis_size("chan")
    pairs = []
    for brick in range(bricks):
        for chan in range(chans):
            other = brick_partner(kind, brick, bricks)
            target = chan if chan_of is None else chan_of(chan)
            if other is None and chans % 2 == 0:
                other, target = brick, chan ^ 1
            if other is not None and 0 <= target < chans:
                pairs.append((brick * chans + chan, other * chans + target))
    return lax.ppermute(value, AXES, pairs)


def has_far():
    brick = lax.axis_index("brick")
    edge = brick + lax.rem(brick, 2)
    return jnp.logical_and(edge > 0, edge < lax.axis_size("brick"))


def early(out):
    out[...] = jnp.zeros_like(out)


def edge_rows(volume, _, *edges, chans):
    size_y = volume.shape[1]
    starts = [jnp.where(lax.axis_index("chan") == 0, size_y - 2, 0)] if chans == 2 else [size_y - 2, 0]
    for edge, start in zip(edges, starts):
        edge[...] = volume[:, pl.ds(start, 2)]


def call(kernel, inputs, outputs, scratch, flops, limit_mib, results_in_vmem=True):
    inputs = [pltpu.with_memory_space_constraint(value, pltpu.VMEM) for value in inputs]
    if results_in_vmem:
        out_shape = [pltpu.VMEM(shape, dtype) for shape, dtype in outputs]
    else:
        out_shape = [jax.ShapeDtypeStruct(shape, dtype) for shape, dtype in outputs]
    return pl.pallas_call(
        kernel,
        out_shape=out_shape,
        in_specs=[VMEM_SPEC] * len(inputs),
        out_specs=[VMEM_SPEC] * len(outputs),
        scratch_shapes=scratch,
        compiler_params=pltpu.CompilerParams(vmem_limit_bytes=limit_mib * 2**20),
        cost_estimate=pl.CostEstimate(flops=flops, bytes_accessed=2**20, transcendentals=0),
    )(*inputs)


def tile_of(rows):
    return max(lines for lines in range(1, 10) if rows % lines == 0)


def conv_lines(terms, row, lines, weight):
    sums = []
    for dz in range(3):
        total = None
        for ref, plane, dx in terms:
            for dy in range(3):
                window = ref[plane, pl.ds(row + dy, lines)]
                window = window.reshape(lines * window.shape[1], window.shape[2])
                part = jnp.dot(window, weight[dx, dy, dz], preferred_element_type=F32)
                total = part if total is None else total + part
        sums.append(total)
    depth = terms[0][0].shape[2]
    count = sums[0].shape[0]
    place = lax.rem(lax.broadcasted_iota(jnp.int32, sums[0].shape, 0), depth)
    before = jnp.where(place == 0, 0.0, pltpu.roll(sums[0], 1, 0))
    after = jnp.where(place == depth - 1, 0.0, pltpu.roll(sums[2], count - 1, 0))
    return (before + sums[1] + after).reshape(lines, depth, sums[0].shape[1])


def tap(step, odd):
    return step + odd * (2 - 2 * step)


def halo_plan(chans, size_y):
    chan = lax.axis_index("chan")
    if chans == 1:
        return []
    if chans == 2:
        return [(jnp.where(chan == 1, 0, size_y + 2), jnp.where(chan == 1, size_y + 2, 0))]
    return [(0, None), (size_y + 2, None)]


def fill_planes(target, slot, plane, block, halos, chans, valid=None):
    def rows_of(ref):
        rows = ref[plane]
        return rows if valid is None else jnp.where(valid, rows, jnp.zeros_like(rows))

    size_y = block.shape[1]
    target[slot, 2 : size_y + 2] = rows_of(block)
    zeros = jnp.zeros((2,) + target.shape[2:], target.dtype)
    if chans == 1:
        target[slot, 0:2] = zeros
        target[slot, size_y + 2 : size_y + 4] = zeros
    for (place, empty), halo in zip(halo_plan(chans, size_y), halos):
        target[slot, pl.ds(place, 2)] = rows_of(halo)
        if empty is not None:
            target[slot, pl.ds(empty, 2)] = zeros


def first_row(chans):
    if chans == 1:
        return 0
    if chans == 2:
        return -lax.axis_index("chan")
    return -1


def clear_outside(layer, slot, chans):
    chan = lax.axis_index("chan")
    last = layer.shape[1] - 1
    for row, owner in ((0, 0), (last, chans - 1)):
        if chans <= 2:
            keep = jnp.logical_and(chans == 2, chan != owner)
        else:
            keep = chan != owner
        layer[slot, row] = jnp.where(keep, layer[slot, row], jnp.zeros_like(layer[slot, row]))


def kernel_a(*refs, chans, halo_count):
    own, own_halos = refs[0], refs[1 : 1 + halo_count]
    near, near_halos = refs[1 + halo_count], refs[2 + halo_count : 2 + 2 * halo_count]
    weight_one, weight_two, layer_far, layer_own, out_far, out_near, field, layer = refs[2 + 2 * halo_count :]
    odd = lax.rem(lax.axis_index("brick"), 2)
    size_y = own.shape[1]
    fill_planes(field, 0, odd, own, own_halos, chans)
    fill_planes(field, 1, 1 - odd, own, own_halos, chans)
    fill_planes(field, 2, odd, near, near_halos, chans)
    fill_planes(field, 3, 1 - odd, near, near_halos, chans)
    start = first_row(chans)
    rows = layer_far.shape[0]
    lines = tile_of(rows)
    for row in range(0, rows, lines):
        base = start + row + 1
        for slot in range(2):
            terms = [(field, slot + step, tap(step, odd)) for step in range(3)]
            value = jnp.maximum(conv_lines(terms, base, lines, weight_one), 0.0).astype(BF16)
            layer[slot, pl.ds(start + row + 1, lines)] = value
    for slot in range(2):
        clear_outside(layer, slot, chans)
    lines_out = tile_of(size_y)
    for row in range(0, size_y, lines_out):
        out_far[pl.ds(row, lines_out)] = conv_lines([(layer, 0, tap(2, odd))], row, lines_out, weight_two)
        out_near[pl.ds(row, lines_out)] = conv_lines(
            [(layer, 0, tap(1, odd)), (layer, 1, tap(2, odd))], row, lines_out, weight_two
        )
    for row in range(0, rows, lines):
        base = start + row + 1
        layer_own[pl.ds(row, lines)] = conv_lines(
            [(field, 0, tap(1, odd)), (field, 1, tap(2, odd))], base, lines, weight_one
        )
        layer_far[pl.ds(row, lines)] = conv_lines([(field, 0, tap(2, odd))], base, lines, weight_one)


def kernel_b(*refs, chans, halo_count):
    far, far_halos = refs[0], refs[1 : 1 + halo_count]
    layer_far, layer_own, out_far, out_near, weight_one, weight_two = refs[1 + halo_count : 7 + halo_count]
    skipped, pooled, field, layer, sums = refs[7 + halo_count :]
    odd = lax.rem(lax.axis_index("brick"), 2)
    size_y, depth = out_far.shape[0], out_far.shape[1]
    inside = has_far()
    fill_planes(field, 0, odd, far, far_halos, chans, inside)
    fill_planes(field, 1, 1 - odd, far, far_halos, chans, inside)
    start = first_row(chans)
    rows = layer_far.shape[0]
    lines = tile_of(rows)
    for row in range(0, rows, lines):
        base = start + row + 1
        value = conv_lines([(field, 0, tap(0, odd)), (field, 1, tap(1, odd))], base, lines, weight_one)
        value = jnp.maximum(value + layer_far[pl.ds(row, lines)], 0.0)
        layer[0, pl.ds(base, lines)] = jnp.where(inside, value, 0.0).astype(BF16)
        value = conv_lines([(field, 1, tap(0, odd))], base, lines, weight_one)
        value = jnp.maximum(value + layer_own[pl.ds(row, lines)], 0.0)
        layer[1, pl.ds(base, lines)] = value.astype(BF16)
    for slot in range(2):
        clear_outside(layer, slot, chans)
    lines_out = tile_of(size_y)
    for row in range(0, size_y, lines_out):
        spot = pl.ds(row, lines_out)
        value = conv_lines([(layer, 0, tap(0, odd)), (layer, 1, tap(1, odd))], row, lines_out, weight_two)
        first = jnp.maximum(value + out_far[spot], 0.0).astype(BF16)
        skipped[odd, spot] = first
        value = conv_lines([(layer, 1, tap(0, odd))], row, lines_out, weight_two)
        second = jnp.maximum(value + out_near[spot], 0.0).astype(BF16)
        skipped[1 - odd, spot] = second
        both = first.astype(F32) + second.astype(F32)
        for group in range(sums.shape[0]):
            sums[group, spot] = both[:, :, group * LANES : (group + 1) * LANES]
    for row in range(size_y // 2):
        for group in range(sums.shape[0]):
            pairs = [
                sums[group, 2 * row + step, pl.ds(side, depth // 2, stride=2)] for step in range(2) for side in range(2)
            ]
            mean = (pairs[0] + pairs[1] + pairs[2] + pairs[3]) * 0.125
            pooled[row, :, group * LANES : (group + 1) * LANES] = mean.astype(BF16)


def kernel_c(*refs, chans):
    blocks = refs[: 3 * chans]
    weight, projection = refs[3 * chans : 3 * chans + 2]
    own_part, sent = refs[3 * chans + 2], refs[3 * chans + 3 : 4 * chans + 2]
    field, parts = refs[4 * chans + 2 :]
    odd = lax.rem(lax.axis_index("brick"), 2)
    chan = lax.axis_index("chan")
    rows, depth = blocks[0].shape[0], blocks[0].shape[1]
    total = chans * rows
    inside = has_far()
    for plane in range(3):
        zeros = jnp.zeros(field.shape[2:], field.dtype)
        field[plane, 0] = zeros
        field[plane, total + 1] = zeros
        for step in range(chans):
            source = lax.rem(chan - step + chans, chans)
            block = blocks[plane * chans + step][...]
            if plane == 0:
                block = jnp.where(inside, block, jnp.zeros_like(block))
            field[plane, pl.ds(1 + source * rows, rows)] = block
    lines = tile_of(total)
    for row in range(0, total, lines):
        value = conv_lines([(field, step, tap(step, odd)) for step in range(3)], row, lines, weight)
        value = jnp.maximum(value, 0.0).astype(BF16).reshape(lines * depth, weight.shape[4])
        part = jnp.dot(value, projection[...], preferred_element_type=F32)
        parts[pl.ds(row, lines)] = part.reshape(lines, depth, part.shape[1])
    own_part[...] = parts[pl.ds(chan * rows, rows)]
    for step in range(1, chans):
        target = lax.rem(chan + step, chans)
        sent[step - 1][...] = parts[pl.ds(target * rows, rows)].astype(BF16)


def kernel_d(*refs):
    skipped, own_part = refs[0], refs[1]
    received, merged, fine = refs[2:-2], refs[-2], refs[-1]
    rows, depth = own_part.shape[0], own_part.shape[1]
    lifted = own_part[...]
    for part in received:
        lifted = lifted + part[...].astype(F32)
    for group in range(fine.shape[0]):
        lanes = slice(group * LANES, (group + 1) * LANES)
        for row in range(rows):
            for side in range(2):
                fine[group, row, pl.ds(side, depth, stride=2)] = lifted[row, :, lanes]
        for row in range(rows):
            value = fine[group, row]
            for plane in range(2):
                for step in range(2):
                    line = 2 * row + step
                    merged[plane, line, :, lanes] = (skipped[plane, line, :, lanes].astype(F32) + value).astype(BF16)


def shards(volume, first_weight, second_weight, coarse_weight, projection):
    chans = lax.axis_size("chan")
    size_x, size_y, depth, channels = volume.shape
    assert size_x == 2 and lax.axis_size("brick") % 2 == 0

    turns = [[], [lambda c: 1 - c]][chans - 1] if chans <= 2 else [lambda c: c + 1, lambda c: c - 1]
    far = exchange(volume, "far")
    near = exchange(volume, "near")
    edges = []
    if chans > 1:
        token = call(early, [], [((8, LANES), F32)], [], WEIGHT_COPY_FLOPS, 4)[0]
        edges = call(
            functools.partial(edge_rows, chans=chans),
            [volume, token],
            [((2, 2, depth, channels), BF16)] * len(turns),
            [],
            WEIGHT_COPY_FLOPS,
            4,
        )
    own_halos = [exchange(edge, "own", turn) for edge, turn in zip(edges, turns)]
    far_halos = [exchange(halo, "far") for halo in own_halos]
    near_halos = [exchange(halo, "near") for halo in own_halos]

    rows = size_y + min(chans - 1, 2)
    flops_of_plane = 2 * size_y * depth * 9 * channels * channels
    static = dict(chans=chans, halo_count=len(turns))
    partials = call(
        functools.partial(kernel_a, **static),
        [volume, *own_halos, near, *near_halos, first_weight, second_weight],
        [((rows, depth, channels), F32)] * 2 + [((size_y, depth, channels), F32)] * 2,
        [pltpu.VMEM((4, size_y + 4, depth, channels), BF16), pltpu.VMEM((2, size_y + 2, depth, channels), BF16)],
        12 * flops_of_plane,
        16,
    )
    skipped, pooled = call(
        functools.partial(kernel_b, **static),
        [far, *far_halos, *partials, first_weight, second_weight],
        [(volume.shape, BF16), ((size_y // 2, depth // 2, channels), BF16)],
        [
            pltpu.VMEM((2, size_y + 4, depth, channels), BF16),
            pltpu.VMEM((2, size_y + 2, depth, channels), BF16),
            pltpu.VMEM((channels // LANES, size_y, depth, LANES), F32),
        ],
        6 * flops_of_plane,
        16,
    )

    turns = [(lambda c, step=step: (c + step) % chans) for step in range(chans)]
    own_blocks = [pooled] + [exchange(pooled, "own", turn) for turn in turns[1:]]
    far_blocks = [exchange(pooled, "far")]
    far_blocks += [exchange(block, "far") for block in own_blocks[1:]]
    near_blocks = [exchange(pooled, "near")]
    near_blocks += [exchange(block, "near") for block in own_blocks[1:]]
    part_shape = (size_y // 2, depth // 2, channels)
    coarse_rows = chans * size_y // 2
    parts = call(
        functools.partial(kernel_c, chans=chans),
        [*far_blocks, *own_blocks, *near_blocks, coarse_weight, projection],
        [(part_shape, F32)] + [(part_shape, BF16)] * (chans - 1),
        [
            pltpu.VMEM((3, coarse_rows + 2, depth // 2, channels), BF16),
            pltpu.VMEM((coarse_rows, depth // 2, channels), F32),
        ],
        2 * coarse_rows * (depth // 2) * 27 * channels * coarse_weight.shape[4],
        16,
    )
    received = [exchange(part, "own", turn) for part, turn in zip(parts[1:], turns[1:])]
    return call(
        kernel_d,
        [skipped, parts[0], *received],
        [(volume.shape, BF16)],
        [pltpu.VMEM((channels // LANES, size_y // 2, depth, LANES), F32)],
        volume.size,
        16,
        results_in_vmem=False,
    )[0]


def solution(mesh):
    in_specs = (
        P("brick", "chan", None, None),
        P(),
        P(),
        P(None, None, None, None, "chan"),
        P("chan", None),
    )
    out_specs = P("brick", "chan", None, None)

    return jax.shard_map(shards, mesh=mesh, in_specs=in_specs, out_specs=out_specs, check_vma=False)
```

profile of v0, /device:TPU:0, one launch (start us, length us, event | category | flops | bytes accessed | tf_op | source)
XLA Modules:
  0.0 43.5 jit_solution(12172148974184175467)
XLA Ops:
  0.0 0.0 copy-start.4
  0.0 0.5 %collective-permute-start.3 = (bf16[2,8,64,256]{3,2,1,0:T(8,128)(2,1)}, bf16[2,8,64,256]{3,2,1,0:T(8,128)(2,1)S(1)}, u32[]{:S(2)}, u32[]{:S(2)}) collective-permute-start(bf16[2,8,64,256]{3,2,1,0:T(8,128)(2,1)} %refs_0_.1), channel_id=1, source_target_pairs={{0,2},{1,3},{2,0},{3,1},{4,6},{5,7},{6,4},{7,5},{8,10},{9,11},{10,... | collective-permute-start | bytes 1572872 | tf_op jit(solution)/shard_map/ppermute | solution.py:37
  0.5 0.5 %copy-done.4 = bf16[2,8,64,256]{3,2,1,0:T(8,128)(2,1)S(1)} copy-done((bf16[2,8,64,256]{3,2,1,0:T(8,128)(2,1)S(1)}, bf16[2,8,64,256]{3,2,1,0:T(8,128)(2,1)}, u32[]{:S(2)}) %copy-start.4) | copy-done | bytes 524312
  1.1 3.0 %collective-permute-start.1 = (bf16[2,2,64,256]{3,2,1,0:T(8,128)(2,1)S(1)}, bf16[2,2,64,256]{3,2,1,0:T(8,128)(2,1)S(1)}, u32[]{:S(2)}, u32[]{:S(2)}) collective-permute-start(bf16[2,2,64,256]{3,2,1,0:T(8,128)(2,1)S(1)} %shard_map.56), channel_id=1, source_target_pairs={{0,1},{1,0},{2,3},{3,2},{4,5},{5,4},{6,7},{7,6},{8,9},{9,8},{10,11... | collective-permute-start | bytes 393224 | tf_op jit(solution)/shard_map/ppermute | solution.py:37
  4.1 3.5 %collective-permute-done.1.refs_1_ = bf16[2,2,64,256]{3,2,1,0:T(8,128)(2,1)S(1)} collective-permute-done((bf16[2,2,64,256]{3,2,1,0:T(8,128)(2,1)S(1)}, bf16[2,2,64,256]{3,2,1,0:T(8,128)(2,1)S(1)}, u32[]{:S(2)}, u32[]{:S(2)}) %collective-permute-start.1) | collective-permute-done | bytes 131104 | tf_op jit(solution)/shard_map/ppermute | solution.py:37
  7.6 0.0 collective-permute-start.4
  7.6 1.7 %collective-permute-start = (bf16[2,8,64,256]{3,2,1,0:T(8,128)(2,1)S(1)}, bf16[2,8,64,256]{3,2,1,0:T(8,128)(2,1)S(1)}, u32[]{:S(2)}, u32[]{:S(2)}) collective-permute-start(bf16[2,8,64,256]{3,2,1,0:T(8,128)(2,1)S(1)} %copy-done.4), channel_id=1, source_target_pairs={{0,1},{1,0},{2,4},{3,5},{4,2},{5,3},{6,8},{7,9},{8,6},{9,7},{10,12... | collective-permute-start | bytes 1572872 | tf_op jit(solution)/shard_map/ppermute | solution.py:37
  9.3 0.3 collective-permute-start.2
  9.6 0.0 collective-permute-done.4.refs_3_
  9.6 0.0 collective-permute-done.3.refs_2_
  9.6 0.0 copy-done.2
  9.6 0.0 copy-done.3
  9.6 8.4 %shard_map.57 = (f32[9,64,256]{2,1,0:T(8,128)S(1)}, f32[9,64,256]{2,1,0:T(8,128)S(1)}, f32[8,64,256]{2,1,0:T(8,128)S(1)}, f32[8,64,256]{2,1,0:T(8,128)S(1)}) custom-call(bf16[2,8,64,256]{3,2,1,0:T(8,128)(2,1)S(1)} %copy-done.4, bf16[2,2,64,256]{3,2,1,0:T(8,128)(2,1)S(1)} %collective-permute-done.1.refs_1_, ...), custom_call_target="tpu_custom_call" | custom-call | flops 7247757312 | bytes 1048576 | tf_op jit(solution)/shard_map/pallas_call | solution.py:63
  18.0 0.2 collective-permute-done.2.refs_1_
  18.2 0.0 collective-permute-done.refs_0_
  18.2 4.4 %shard_map.58 = (bf16[2,8,64,256]{3,2,1,0:T(8,128)(2,1)S(1)}, bf16[4,32,256]{2,1,0:T(8,128)(2,1)S(1)}) custom-call(bf16[2,8,64,256]{3,2,1,0:T(8,128)(2,1)S(1)} %collective-permute-done.refs_0_, bf16[2,2,64,256]{3,2,1,0:T(8,128)(2,1)S(1)} %collective-permute-done.2.refs_1_, f32[9,64,256]{2,1,0:T(8,128)S(1)} %get-tuple-element.13.refs_2_, ...), custom_call_target="tpu_custom_call" | custom-call | flops 3623878656 | bytes 1048576 | tf_op jit(solution)/shard_map/pallas_call | solution.py:63
  22.6 1.8 %collective-permute-start.6 = (bf16[4,32,256]{2,1,0:T(8,128)(2,1)S(1)}, bf16[4,32,256]{2,1,0:T(8,128)(2,1)S(1)}, u32[]{:S(2)}, u32[]{:S(2)}) collective-permute-start(bf16[4,32,256]{2,1,0:T(8,128)(2,1)S(1)} %get-tuple-element.18.refs_2_), channel_id=1, source_target_pairs={{0,1},{1,0},{2,3},{3,2},{4,5},{5,4},{6,7},{7,6},{8,9},{9,8},{10,11... | collective-permute-start | bytes 196616 | tf_op jit(solution)/shard_map/ppermute | solution.py:37
  24.4 0.3 collective-permute-start.5
  24.7 7.8 %collective-permute-start.8 = (bf16[4,32,256]{2,1,0:T(8,128)(2,1)S(1)}, bf16[4,32,256]{2,1,0:T(8,128)(2,1)S(1)}, u32[]{:S(2)}, u32[]{:S(2)}) collective-permute-start(bf16[4,32,256]{2,1,0:T(8,128)(2,1)S(1)} %get-tuple-element.18.refs_2_), channel_id=1, source_target_pairs={{0,2},{1,3},{2,0},{3,1},{4,6},{5,7},{6,4},{7,5},{8,10},{9,11},{10,... | collective-permute-start | bytes 196616 | tf_op jit(solution)/shard_map/ppermute | solution.py:37
  32.5 0.0 collective-permute-done.6.refs_3_
  32.5 0.5 %collective-permute-start.7 = (bf16[4,32,256]{2,1,0:T(8,128)(2,1)S(1)}, bf16[4,32,256]{2,1,0:T(8,128)(2,1)S(1)}, u32[]{:S(2)}, u32[]{:S(2)}) collective-permute-start(bf16[4,32,256]{2,1,0:T(8,128)(2,1)S(1)} %collective-permute-done.6.refs_3_), channel_id=1, source_target_pairs={{0,1},{1,0},{2,4},{3,5},{4,2},{5,3},{6,8},{7,9},{8,6},{9,7},{10,12... | collective-permute-start | bytes 196616 | tf_op jit(solution)/shard_map/ppermute | solution.py:37
  33.1 2.2 %collective-permute-start.9 = (bf16[4,32,256]{2,1,0:T(8,128)(2,1)S(1)}, bf16[4,32,256]{2,1,0:T(8,128)(2,1)S(1)}, u32[]{:S(2)}, u32[]{:S(2)}) collective-permute-start(bf16[4,32,256]{2,1,0:T(8,128)(2,1)S(1)} %collective-permute-done.6.refs_3_), channel_id=1, source_target_pairs={{0,2},{1,3},{2,0},{3,1},{4,6},{5,7},{6,4},{7,5},{8,10},{9,11},{10,... | collective-permute-start | bytes 196616 | tf_op jit(solution)/shard_map/ppermute | solution.py:37
  35.3 0.0 collective-permute-done.5.refs_0_
  35.3 0.0 collective-permute-done.8.refs_4_
  35.3 1.5 %collective-permute-done.7.refs_1_ = bf16[4,32,256]{2,1,0:T(8,128)(2,1)S(1)} collective-permute-done((bf16[4,32,256]{2,1,0:T(8,128)(2,1)S(1)}, bf16[4,32,256]{2,1,0:T(8,128)(2,1)S(1)}, u32[]{:S(2)}, u32[]{:S(2)}) %collective-permute-start.7) | collective-permute-done | bytes 65568 | tf_op jit(solution)/shard_map/ppermute | solution.py:37
  36.8 0.0 collective-permute-done.9.refs_5_
  36.8 0.0 copy-done
  36.8 0.0 copy-done.1
  36.8 1.3 %shard_map.59 = (f32[4,32,256]{2,1,0:T(8,128)S(1)}, bf16[4,32,256]{2,1,0:T(8,128)(2,1)S(1)}) custom-call(bf16[4,32,256]{2,1,0:T(8,128)(2,1)S(1)} %collective-permute-done.5.refs_0_, bf16[4,32,256]{2,1,0:T(8,128)(2,1)S(1)} %collective-permute-done.7.refs_1_, bf16[4,32,256]{2,1,0:T(8,128)(2,1)S(1)} %get-tuple-element.18.refs_2_, ...), custom_call_target="tpu_custom_call" | custom-call | flops 905969664 | bytes 1048576 | tf_op jit(solution)/shard_map/pallas_call | solution.py:63
  38.1 1.0 %collective-permute-start.10 = (bf16[4,32,256]{2,1,0:T(8,128)(2,1)S(1)}, bf16[4,32,256]{2,1,0:T(8,128)(2,1)S(1)}, u32[]{:S(2)}, u32[]{:S(2)}) collective-permute-start(bf16[4,32,256]{2,1,0:T(8,128)(2,1)S(1)} %get-tuple-element.20), channel_id=1, source_target_pairs={{0,1},{1,0},{2,3},{3,2},{4,5},{5,4},{6,7},{7,6},{8,9},{9,8},{10,11... | collective-permute-start | bytes 196616 | tf_op jit(solution)/shard_map/ppermute | solution.py:37
  39.1 3.6 %collective-permute-done.10.refs_2_ = bf16[4,32,256]{2,1,0:T(8,128)(2,1)S(1)} collective-permute-done((bf16[4,32,256]{2,1,0:T(8,128)(2,1)S(1)}, bf16[4,32,256]{2,1,0:T(8,128)(2,1)S(1)}, u32[]{:S(2)}, u32[]{:S(2)}) %collective-permute-start.10) | collective-permute-done | bytes 65568 | tf_op jit(solution)/shard_map/ppermute | solution.py:37
  42.6 0.9 %shard_map.60 = bf16[2,8,64,256]{3,2,1,0:T(8,128)(2,1)} custom-call(bf16[2,8,64,256]{3,2,1,0:T(8,128)(2,1)S(1)} %get-tuple-element.17.refs_0_, f32[4,32,256]{2,1,0:T(8,128)S(1)} %get-tuple-element.19.refs_1_, bf16[4,32,256]{2,1,0:T(8,128)(2,1)S(1)} %collective-permute-done.10.refs_2_), custom_call_target="tpu_custom_call" | custom-call | flops 262144 | bytes 1048576 | tf_op jit(solution)/shard_map/pallas_call | solution.py:63
  (6 shorter events, 0.0 us)
Async XLA Ops:
  0.0 1.0 %copy-start.4 = (bf16[2,8,64,256]{3,2,1,0:T(8,128)(2,1)S(1)}, bf16[2,8,64,256]{3,2,1,0:T(8,128)(2,1)}, u32[]{:S(2)}) copy-start(bf16[2,8,64,256]{3,2,1,0:T(8,128)(2,1)} %refs_0_.1) | copy-start | bytes 1572868
  0.0 9.6 %collective-permute-start.3 = (bf16[2,8,64,256]{3,2,1,0:T(8,128)(2,1)}, bf16[2,8,64,256]{3,2,1,0:T(8,128)(2,1)S(1)}, u32[]{:S(2)}, u32[]{:S(2)}) collective-permute-start(bf16[2,8,64,256]{3,2,1,0:T(8,128)(2,1)} %refs_0_.1), channel_id=1, source_target_pairs={{0,2},{1,3},{2,0},{3,1},{4,6},{5,7},{6,4},{7,5},{8,10},{9,11},{10,... | collective-permute-start | bytes 1572872 | tf_op jit(solution)/shard_map/ppermute | solution.py:37
  1.0 8.6 %copy-start.2 = (bf16[3,3,3,256,256]{4,3,2,1,0:T(8,128)(2,1)S(1)}, bf16[3,3,3,256,256]{4,3,2,1,0:T(8,128)(2,1)}, u32[]{:S(2)}) copy-start(bf16[3,3,3,256,256]{4,3,2,1,0:T(8,128)(2,1)} %refs_6_.2) | copy-start | bytes 10616836
  1.0 8.6 %copy-start.3 = (bf16[3,3,3,256,256]{4,3,2,1,0:T(8,128)(2,1)S(1)}, bf16[3,3,3,256,256]{4,3,2,1,0:T(8,128)(2,1)}, u32[]{:S(2)}) copy-start(bf16[3,3,3,256,256]{4,3,2,1,0:T(8,128)(2,1)} %refs_7_.2) | copy-start | bytes 10616836
  1.1 6.5 %collective-permute-start.1 = (bf16[2,2,64,256]{3,2,1,0:T(8,128)(2,1)S(1)}, bf16[2,2,64,256]{3,2,1,0:T(8,128)(2,1)S(1)}, u32[]{:S(2)}, u32[]{:S(2)}) collective-permute-start(bf16[2,2,64,256]{3,2,1,0:T(8,128)(2,1)S(1)} %shard_map.56), channel_id=1, source_target_pairs={{0,1},{1,0},{2,3},{3,2},{4,5},{5,4},{6,7},{7,6},{8,9},{9,8},{10,11... | collective-permute-start | bytes 393224 | tf_op jit(solution)/shard_map/ppermute | solution.py:37
  7.6 2.0 %collective-permute-start.4 = (bf16[2,2,64,256]{3,2,1,0:T(8,128)(2,1)S(1)}, bf16[2,2,64,256]{3,2,1,0:T(8,128)(2,1)S(1)}, u32[]{:S(2)}, u32[]{:S(2)}) collective-permute-start(bf16[2,2,64,256]{3,2,1,0:T(8,128)(2,1)S(1)} %collective-permute-done.1.refs_1_), channel_id=1, source_target_pairs={{0,2},{1,3},{2,0},{3,1},{4,6},{5,7},{6,4},{7,5},{8,10},{9,11},{10,... | collective-permute-start | bytes 393224 | tf_op jit(solution)/shard_map/ppermute | solution.py:37
  7.6 10.6 %collective-permute-start = (bf16[2,8,64,256]{3,2,1,0:T(8,128)(2,1)S(1)}, bf16[2,8,64,256]{3,2,1,0:T(8,128)(2,1)S(1)}, u32[]{:S(2)}, u32[]{:S(2)}) collective-permute-start(bf16[2,8,64,256]{3,2,1,0:T(8,128)(2,1)S(1)} %copy-done.4), channel_id=1, source_target_pairs={{0,1},{1,0},{2,4},{3,5},{4,2},{5,3},{6,8},{7,9},{8,6},{9,7},{10,12... | collective-permute-start | bytes 1572872 | tf_op jit(solution)/shard_map/ppermute | solution.py:37
  9.3 8.8 %collective-permute-start.2 = (bf16[2,2,64,256]{3,2,1,0:T(8,128)(2,1)S(1)}, bf16[2,2,64,256]{3,2,1,0:T(8,128)(2,1)S(1)}, u32[]{:S(2)}, u32[]{:S(2)}) collective-permute-start(bf16[2,2,64,256]{3,2,1,0:T(8,128)(2,1)S(1)} %collective-permute-done.1.refs_1_), channel_id=1, source_target_pairs={{0,1},{1,0},{2,4},{3,5},{4,2},{5,3},{6,8},{7,9},{8,6},{9,7},{10,12... | collective-permute-start | bytes 393224 | tf_op jit(solution)/shard_map/ppermute | solution.py:37
  18.2 18.6 %copy-start = (bf16[3,3,3,256,256]{4,3,2,1,0:T(8,128)(2,1)S(1)}, bf16[3,3,3,256,256]{4,3,2,1,0:T(8,128)(2,1)}, u32[]{:S(2)}) copy-start(bf16[3,3,3,256,256]{4,3,2,1,0:T(8,128)(2,1)} %refs_6_.3) | copy-start | bytes 10616836
  18.2 18.6 %copy-start.1 = (bf16[256,256]{1,0:T(8,128)(2,1)S(1)}, bf16[256,256]{1,0:T(8,128)(2,1)}, u32[]{:S(2)}) copy-start(bf16[256,256]{1,0:T(8,128)(2,1)} %refs_7_.3) | copy-start | bytes 393220
  22.6 9.9 %collective-permute-start.6 = (bf16[4,32,256]{2,1,0:T(8,128)(2,1)S(1)}, bf16[4,32,256]{2,1,0:T(8,128)(2,1)S(1)}, u32[]{:S(2)}, u32[]{:S(2)}) collective-permute-start(bf16[4,32,256]{2,1,0:T(8,128)(2,1)S(1)} %get-tuple-element.18.refs_2_), channel_id=1, source_target_pairs={{0,1},{1,0},{2,3},{3,2},{4,5},{5,4},{6,7},{7,6},{8,9},{9,8},{10,11... | collective-permute-start | bytes 196616 | tf_op jit(solution)/shard_map/ppermute | solution.py:37
  24.4 10.9 %collective-permute-start.5 = (bf16[4,32,256]{2,1,0:T(8,128)(2,1)S(1)}, bf16[4,32,256]{2,1,0:T(8,128)(2,1)S(1)}, u32[]{:S(2)}, u32[]{:S(2)}) collective-permute-start(bf16[4,32,256]{2,1,0:T(8,128)(2,1)S(1)} %get-tuple-element.18.refs_2_), channel_id=1, source_target_pairs={{0,1},{1,0},{2,4},{3,5},{4,2},{5,3},{6,8},{7,9},{8,6},{9,7},{10,12... | collective-permute-start | bytes 196616 | tf_op jit(solution)/shard_map/ppermute | solution.py:37
  24.7 10.6 %collective-permute-start.8 = (bf16[4,32,256]{2,1,0:T(8,128)(2,1)S(1)}, bf16[4,32,256]{2,1,0:T(8,128)(2,1)S(1)}, u32[]{:S(2)}, u32[]{:S(2)}) collective-permute-start(bf16[4,32,256]{2,1,0:T(8,128)(2,1)S(1)} %get-tuple-element.18.refs_2_), channel_id=1, source_target_pairs={{0,2},{1,3},{2,0},{3,1},{4,6},{5,7},{6,4},{7,5},{8,10},{9,11},{10,... | collective-permute-start | bytes 196616 | tf_op jit(solution)/shard_map/ppermute | solution.py:37
  32.5 4.3 %collective-permute-start.7 = (bf16[4,32,256]{2,1,0:T(8,128)(2,1)S(1)}, bf16[4,32,256]{2,1,0:T(8,128)(2,1)S(1)}, u32[]{:S(2)}, u32[]{:S(2)}) collective-permute-start(bf16[4,32,256]{2,1,0:T(8,128)(2,1)S(1)} %collective-permute-done.6.refs_3_), channel_id=1, source_target_pairs={{0,1},{1,0},{2,4},{3,5},{4,2},{5,3},{6,8},{7,9},{8,6},{9,7},{10,12... | collective-permute-start | bytes 196616 | tf_op jit(solution)/shard_map/ppermute | solution.py:37
  33.1 3.7 %collective-permute-start.9 = (bf16[4,32,256]{2,1,0:T(8,128)(2,1)S(1)}, bf16[4,32,256]{2,1,0:T(8,128)(2,1)S(1)}, u32[]{:S(2)}, u32[]{:S(2)}) collective-permute-start(bf16[4,32,256]{2,1,0:T(8,128)(2,1)S(1)} %collective-permute-done.6.refs_3_), channel_id=1, source_target_pairs={{0,2},{1,3},{2,0},{3,1},{4,6},{5,7},{6,4},{7,5},{8,10},{9,11},{10,... | collective-permute-start | bytes 196616 | tf_op jit(solution)/shard_map/ppermute | solution.py:37
  38.1 4.5 %collective-permute-start.10 = (bf16[4,32,256]{2,1,0:T(8,128)(2,1)S(1)}, bf16[4,32,256]{2,1,0:T(8,128)(2,1)S(1)}, u32[]{:S(2)}, u32[]{:S(2)}) collective-permute-start(bf16[4,32,256]{2,1,0:T(8,128)(2,1)S(1)} %get-tuple-element.20), channel_id=1, source_target_pairs={{0,1},{1,0},{2,3},{3,2},{4,5},{5,4},{6,7},{7,6},{8,9},{9,8},{10,11... | collective-permute-start | bytes 196616 | tf_op jit(solution)/shard_map/ppermute | solution.py:37
where the time goes:
time: 43.7 us; the launch traced here: 43.5 us
  starting transfers between devices  19.2 us (44%)
  Pallas kernels  15 us (34%)
  waiting for transfers between devices  8.74 us (20%)
  local copies, waits for them, and re-layouts  0.56 us (1%)
    ppermute x11, starting transfers between devices, exchange(): return lax.ppermute(value, AXES, pairs)  19.2 us
    pallas_call x6, Pallas kernels, call(): pl.pallas_call(kernel, out_shape=out_shape, in_specs=[VMEM_SPEC] * len(in...  15 us
    ppermute x11, waiting for transfers between devices, exchange(): return lax.ppermute(value, AXES, pairs)  8.74 us
  transfers between devices with their start and end apart: 11, of which 4 were waited for; matrix products, arithmetic and copies ran while one was open for 0% of the time, Pallas kernels for 19%

commit v1 on v0

--- a/solution.py
+++ b/solution.py
@@ -47,8 +47,11 @@
     out[...] = jnp.zeros_like(out)
 
 
-def edge_rows(volume, _, *edges, chans):
+def pieces_to_send(volume, _, first, second, *edges, chans):
+    odd = lax.rem(lax.axis_index("brick"), 2)
     size_y = volume.shape[1]
+    first[...] = volume[odd]
+    second[...] = volume[1 - odd]
     starts = [jnp.where(lax.axis_index("chan") == 0, size_y - 2, 0)] if chans == 2 else [size_y - 2, 0]
     for edge, start in zip(edges, starts):
         edge[...] = volume[:, pl.ds(start, 2)]
@@ -107,29 +110,38 @@
     return [(0, None), (size_y + 2, None)]
 
 
-def fill_planes(target, slot, plane, block, halos, chans, valid=None):
-    def rows_of(ref):
-        rows = ref[plane]
-        return rows if valid is None else jnp.where(valid, rows, jnp.zeros_like(rows))
-
-    size_y = block.shape[1]
-    target[slot, 2 : size_y + 2] = rows_of(block)
+def inner_rows(chans, size_y):
+    return {1: (0, size_y), 2: (lax.axis_index("chan"), size_y - 1)}.get(chans, (1, size_y - 2))
+
+
+def border_rows(chans, size_y):
+    if chans == 1:
+        return []
+    if chans == 2:
+        return [(jnp.where(lax.axis_index("chan") == 0, size_y - 1, -1), 2)]
+    return [(-1, 2), (size_y - 1, 2)]
+
+
+def row_groups(chans, size_y):
+    return [inner_rows(chans, size_y), *border_rows(chans, size_y)]
+
+
+def fill_plane(target, block, plane, halos, chans):
+    valid = has_far()
+
+    def masked(rows):
+        return jnp.where(valid, rows, jnp.zeros_like(rows))
+
+    size_y = block.shape[0]
+    target[0, 2 : size_y + 2] = masked(block[...])
     zeros = jnp.zeros((2,) + target.shape[2:], target.dtype)
     if chans == 1:
-        target[slot, 0:2] = zeros
-        target[slot, size_y + 2 : size_y + 4] = zeros
+        target[0, 0:2] = zeros
+        target[0, size_y + 2 : size_y + 4] = zeros
     for (place, empty), halo in zip(halo_plan(chans, size_y), halos):
-        target[slot, pl.ds(place, 2)] = rows_of(halo)
+        target[0, pl.ds(place, 2)] = masked(halo[plane])
         if empty is not None:
-            target[slot, pl.ds(empty, 2)] = zeros
-
-
-def first_row(chans):
-    if chans == 1:
-        return 0
-    if chans == 2:
-        return -lax.axis_index("chan")
-    return -1
+            target[0, pl.ds(empty, 2)] = zeros
 
 
 def clear_outside(layer, slot, chans):
@@ -143,73 +155,110 @@
         layer[slot, row] = jnp.where(keep, layer[slot, row], jnp.zeros_like(layer[slot, row]))
 
 
-def kernel_a(*refs, chans, halo_count):
-    own, own_halos = refs[0], refs[1 : 1 + halo_count]
-    near, near_halos = refs[1 + halo_count], refs[2 + halo_count : 2 + 2 * halo_count]
-    weight_one, weight_two, layer_far, layer_own, out_far, out_near, field, layer = refs[2 + 2 * halo_count :]
+def kernel_a0(own, near, weight_one, done_three, done_four, part_one, part_two, field, *, chans):
     odd = lax.rem(lax.axis_index("brick"), 2)
     size_y = own.shape[1]
-    fill_planes(field, 0, odd, own, own_halos, chans)
-    fill_planes(field, 1, 1 - odd, own, own_halos, chans)
-    fill_planes(field, 2, odd, near, near_halos, chans)
-    fill_planes(field, 3, 1 - odd, near, near_halos, chans)
-    start = first_row(chans)
-    rows = layer_far.shape[0]
+    zeros = jnp.zeros(field.shape[2:], field.dtype)
+    for slot, (block, plane) in enumerate(((own, odd), (own, 1 - odd), (near, odd), (near, 1 - odd))):
+        field[slot, 0] = zeros
+        field[slot, 1 : size_y + 1] = block[plane]
+        field[slot, size_y + 1] = zeros
+    first, rows = inner_rows(chans, size_y)
     lines = tile_of(rows)
     for row in range(0, rows, lines):
-        base = start + row + 1
+        spot, base = pl.ds(row, lines), first + row
+        for slot, done in enumerate((done_three, done_four)):
+            terms = [(field, slot + step, tap(step, odd)) for step in range(3)]
+            done[spot] = jnp.maximum(conv_lines(terms, base, lines, weight_one), 0.0).astype(BF16)
+        terms = [(field, 0, tap(1, odd)), (field, 1, tap(2, odd))]
+        part_two[spot] = conv_lines(terms, base, lines, weight_one)
+        part_one[spot] = conv_lines([(field, 0, tap(2, odd))], base, lines, weight_one)
+
+
+def kernel_a1(*refs, chans, sides):
+    own, own_halos = refs[0], refs[1 : 1 + sides]
+    near, near_halos = refs[1 + sides], refs[2 + sides : 2 + 2 * sides]
+    done_three, done_four, weight_one, weight_two = refs[2 + 2 * sides : 6 + 2 * sides]
+    out_two, out_three = refs[6 + 2 * sides : 8 + 2 * sides]
+    parts = refs[8 + 2 * sides : 8 + 4 * sides]
+    field, layer = refs[8 + 4 * sides :]
+    odd = lax.rem(lax.axis_index("brick"), 2)
+    size_y = own.shape[1]
+    first, rows = inner_rows(chans, size_y)
+    layer[0, pl.ds(first + 1, rows)] = done_three[...]
+    layer[1, pl.ds(first + 1, rows)] = done_four[...]
+    for side, (start, count) in enumerate(border_rows(chans, size_y)):
+        high = start > 0
+        place, source = jnp.where(high, 0, 2), jnp.where(high, size_y - 2, 0)
+        planes = ((own, own_halos, odd), (own, own_halos, 1 - odd), (near, near_halos, odd), (near, near_halos, 1 - odd))
+        for slot, (block, halos, plane) in enumerate(planes):
+            field[slot, pl.ds(place, 2)] = block[plane, pl.ds(source, 2)]
+            field[slot, pl.ds(2 - place, 2)] = halos[side][plane]
         for slot in range(2):
             terms = [(field, slot + step, tap(step, odd)) for step in range(3)]
-            value = jnp.maximum(conv_lines(terms, base, lines, weight_one), 0.0).astype(BF16)
-            layer[slot, pl.ds(start + row + 1, lines)] = value
+            value = jnp.maximum(conv_lines(terms, 0, count, weight_one), 0.0).astype(BF16)
+            layer[slot, pl.ds(start + 1, count)] = value
+        terms = [(field, 0, tap(1, odd)), (field, 1, tap(2, odd))]
+        parts[sides + side][...] = conv_lines(terms, 0, count, weight_one)
+        parts[side][...] = conv_lines([(field, 0, tap(2, odd))], 0, count, weight_one)
     for slot in range(2):
         clear_outside(layer, slot, chans)
-    lines_out = tile_of(size_y)
-    for row in range(0, size_y, lines_out):
-        out_far[pl.ds(row, lines_out)] = conv_lines([(layer, 0, tap(2, odd))], row, lines_out, weight_two)
-        out_near[pl.ds(row, lines_out)] = conv_lines(
-            [(layer, 0, tap(1, odd)), (layer, 1, tap(2, odd))], row, lines_out, weight_two
-        )
-    for row in range(0, rows, lines):
-        base = start + row + 1
-        layer_own[pl.ds(row, lines)] = conv_lines(
-            [(field, 0, tap(1, odd)), (field, 1, tap(2, odd))], base, lines, weight_one
-        )
-        layer_far[pl.ds(row, lines)] = conv_lines([(field, 0, tap(2, odd))], base, lines, weight_one)
-
-
-def kernel_b(*refs, chans, halo_count):
-    far, far_halos = refs[0], refs[1 : 1 + halo_count]
-    layer_far, layer_own, out_far, out_near, weight_one, weight_two = refs[1 + halo_count : 7 + halo_count]
-    skipped, pooled, field, layer, sums = refs[7 + halo_count :]
-    odd = lax.rem(lax.axis_index("brick"), 2)
-    size_y, depth = out_far.shape[0], out_far.shape[1]
+    lines = tile_of(size_y)
+    for row in range(0, size_y, lines):
+        spot = pl.ds(row, lines)
+        out_two[spot] = conv_lines([(layer, 0, tap(2, odd))], row, lines, weight_two)
+        out_three[spot] = conv_lines([(layer, 0, tap(1, odd)), (layer, 1, tap(2, odd))], row, lines, weight_two)
+
+
+def kernel_b1(*refs, chans, sides):
+    block, halos, refs = refs[0], refs[1 : 1 + sides], refs[1 + sides :]
+    part_one, part_two, out_two, out_three, weight_one, weight_two = refs[0], refs[1], *refs[2 + 2 * sides : 6 + 2 * sides]
+    ones, twos = [part_one, *refs[2 : 2 + sides]], [part_two, *refs[2 + sides : 2 + 2 * sides]]
+    refs = refs[6 + 2 * sides :]
+    skipped, more_two, mores = refs[0], refs[1], refs[2 : 3 + sides]
+    field, layer = refs[3 + sides :]
+    odd = lax.rem(lax.axis_index("brick"), 2)
+    size_y = block.shape[0]
+    fill_plane(field, block, 1 - odd, halos, chans)
+    for (start, rows), one, two, more in zip(row_groups(chans, size_y), ones, twos, mores):
+        lines = tile_of(rows)
+        for row in range(0, rows, lines):
+            spot, base = pl.ds(row, lines), start + row + 1
+            value = conv_lines([(field, 0, tap(0, odd))], base, lines, weight_one)
+            layer[0, pl.ds(base, lines)] = jnp.maximum(value + two[spot], 0.0).astype(BF16)
+            more[spot] = one[spot] + conv_lines([(field, 0, tap(1, odd))], base, lines, weight_one)
+    clear_outside(layer, 0, chans)
+    lines = tile_of(size_y)
+    for row in range(0, size_y, lines):
+        spot = pl.ds(row, lines)
+        value = conv_lines([(layer, 0, tap(0, odd))], row, lines, weight_two)
+        skipped[spot] = jnp.maximum(value + out_three[spot], 0.0).astype(BF16)
+        more_two[spot] = out_two[spot] + conv_lines([(layer, 0, tap(1, odd))], row, lines, weight_two)
+
+
+def kernel_b2(*refs, chans, sides):
+    block, halos, refs = refs[0], refs[1 : 1 + sides], refs[1 + sides :]
+    other, out_two, mores, weight_one, weight_two = refs[0], refs[1], refs[2 : 3 + sides], *refs[3 + sides : 5 + sides]
+    skipped, pooled, field, layer, sums = refs[5 + sides :]
+    odd = lax.rem(lax.axis_index("brick"), 2)
     inside = has_far()
-    fill_planes(field, 0, odd, far, far_halos, chans, inside)
-    fill_planes(field, 1, 1 - odd, far, far_halos, chans, inside)
-    start = first_row(chans)
-    rows = layer_far.shape[0]
-    lines = tile_of(rows)
-    for row in range(0, rows, lines):
-        base = start + row + 1
-        value = conv_lines([(field, 0, tap(0, odd)), (field, 1, tap(1, odd))], base, lines, weight_one)
-        value = jnp.maximum(value + layer_far[pl.ds(row, lines)], 0.0)
-        layer[0, pl.ds(base, lines)] = jnp.where(inside, value, 0.0).astype(BF16)
-        value = conv_lines([(field, 1, tap(0, odd))], base, lines, weight_one)
-        value = jnp.maximum(value + layer_own[pl.ds(row, lines)], 0.0)
-        layer[1, pl.ds(base, lines)] = value.astype(BF16)
-    for slot in range(2):
-        clear_outside(layer, slot, chans)
-    lines_out = tile_of(size_y)
-    for row in range(0, size_y, lines_out):
-        spot = pl.ds(row, lines_out)
-        value = conv_lines([(layer, 0, tap(0, odd)), (layer, 1, tap(1, odd))], row, lines_out, weight_two)
-        first = jnp.maximum(value + out_far[spot], 0.0).astype(BF16)
-        skipped[odd, spot] = first
-        value = conv_lines([(layer, 1, tap(0, odd))], row, lines_out, weight_two)
-        second = jnp.maximum(value + out_near[spot], 0.0).astype(BF16)
-        skipped[1 - odd, spot] = second
-        both = first.astype(F32) + second.astype(F32)
+    size_y, depth = block.shape[0], block.shape[1]
+    fill_plane(field, block, odd, halos, chans)
+    for (start, rows), more in zip(row_groups(chans, size_y), mores):
+        lines = tile_of(rows)
+        for row in range(0, rows, lines):
+            base = start + row + 1
+            value = conv_lines([(field, 0, tap(0, odd))], base, lines, weight_one)
+            value = jnp.maximum(value + more[pl.ds(row, lines)], 0.0)
+            layer[0, pl.ds(base, lines)] = jnp.where(inside, value, 0.0).astype(BF16)
+    clear_outside(layer, 0, chans)
+    lines = tile_of(size_y)
+    for row in range(0, size_y, lines):
+        spot = pl.ds(row, lines)
+        value = conv_lines([(layer, 0, tap(0, odd))], row, lines, weight_two)
+        value = jnp.maximum(value + out_two[spot], 0.0).astype(BF16)
+        skipped[spot] = value
+        both = value.astype(F32) + other[spot].astype(F32)
         for group in range(sums.shape[0]):
             sums[group, spot] = both[:, :, group * LANES : (group + 1) * LANES]
     for row in range(size_y // 2):
@@ -254,8 +303,9 @@
 
 
 def kernel_d(*refs):
-    skipped, own_part = refs[0], refs[1]
-    received, merged, fine = refs[2:-2], refs[-2], refs[-1]
+    skipped_two, skipped_three, own_part = refs[:3]
+    received, merged, fine = refs[3:-2], refs[-2], refs[-1]
+    odd = lax.rem(lax.axis_index("brick"), 2)
     rows, depth = own_part.shape[0], own_part.shape[1]
     lifted = own_part[...]
     for part in received:
@@ -267,10 +317,10 @@
                 fine[group, row, pl.ds(side, depth, stride=2)] = lifted[row, :, lanes]
         for row in range(rows):
             value = fine[group, row]
-            for plane in range(2):
+            for plane, skipped in ((odd, skipped_two), (1 - odd, skipped_three)):
                 for step in range(2):
                     line = 2 * row + step
-                    merged[plane, line, :, lanes] = (skipped[plane, line, :, lanes].astype(F32) + value).astype(BF16)
+                    merged[plane, line, :, lanes] = (skipped[line, :, lanes].astype(F32) + value).astype(BF16)
 
 
 def shards(volume, first_weight, second_weight, coarse_weight, projection):
@@ -279,51 +329,66 @@
     assert size_x == 2 and lax.axis_size("brick") % 2 == 0
 
     turns = [[], [lambda c: 1 - c]][chans - 1] if chans <= 2 else [lambda c: c + 1, lambda c: c - 1]
-    far = exchange(volume, "far")
     near = exchange(volume, "near")
-    edges = []
-    if chans > 1:
-        token = call(early, [], [((8, LANES), F32)], [], WEIGHT_COPY_FLOPS, 4)[0]
-        edges = call(
-            functools.partial(edge_rows, chans=chans),
-            [volume, token],
-            [((2, 2, depth, channels), BF16)] * len(turns),
-            [],
-            WEIGHT_COPY_FLOPS,
-            4,
-        )
+    token = call(early, [], [((8, LANES), F32)], [], WEIGHT_COPY_FLOPS, 4)[0]
+    plane_shape, sides = (size_y, depth, channels), len(turns)
+    first, second, *edges = call(
+        functools.partial(pieces_to_send, chans=chans),
+        [volume, token],
+        [(plane_shape, BF16)] * 2 + [((2, 2, depth, channels), BF16)] * sides,
+        [],
+        WEIGHT_COPY_FLOPS,
+        4,
+    )
     own_halos = [exchange(edge, "own", turn) for edge, turn in zip(edges, turns)]
+    far_one = exchange(first, "far")
     far_halos = [exchange(halo, "far") for halo in own_halos]
+    far_zero = exchange(second, "far")
     near_halos = [exchange(halo, "near") for halo in own_halos]
 
-    rows = size_y + min(chans - 1, 2)
-    flops_of_plane = 2 * size_y * depth * 9 * channels * channels
-    static = dict(chans=chans, halo_count=len(turns))
-    partials = call(
-        functools.partial(kernel_a, **static),
-        [volume, *own_halos, near, *near_halos, first_weight, second_weight],
-        [((rows, depth, channels), F32)] * 2 + [((size_y, depth, channels), F32)] * 2,
-        [pltpu.VMEM((4, size_y + 4, depth, channels), BF16), pltpu.VMEM((2, size_y + 2, depth, channels), BF16)],
-        12 * flops_of_plane,
-        16,
-    )
-    skipped, pooled = call(
-        functools.partial(kernel_b, **static),
-        [far, *far_halos, *partials, first_weight, second_weight],
-        [(volume.shape, BF16), ((size_y // 2, depth // 2, channels), BF16)],
-        [
-            pltpu.VMEM((2, size_y + 4, depth, channels), BF16),
-            pltpu.VMEM((2, size_y + 2, depth, channels), BF16),
-            pltpu.VMEM((channels // LANES, size_y, depth, LANES), F32),
-        ],
-        6 * flops_of_plane,
-        16,
+    static = dict(chans=chans, sides=sides)
+    inner = inner_rows(chans, size_y)[1]
+    border_shape = (2, depth, channels)
+    line_flops = 2 * depth * 9 * channels * channels
+    field_of_plane = pltpu.VMEM((1, size_y + 4, depth, channels), BF16)
+    layer_of_plane = pltpu.VMEM((1, size_y + 2, depth, channels), BF16)
+    done_three, done_four, part_one, part_two = call(
+        functools.partial(kernel_a0, chans=chans),
+        [volume, near, first_weight],
+        [((inner, depth, channels), BF16)] * 2 + [((inner, depth, channels), F32)] * 2,
+        [pltpu.VMEM((4, size_y + 2, depth, channels), BF16)],
+        9 * inner * line_flops,
+        12,
+    )
+    out_two, out_three, *border = call(
+        functools.partial(kernel_a1, **static),
+        [volume, *own_halos, near, *near_halos, done_three, done_four, first_weight, second_weight],
+        [(plane_shape, F32)] * 2 + [(border_shape, F32)] * (2 * sides),
+        [pltpu.VMEM((4, 4, depth, channels), BF16), pltpu.VMEM((2, size_y + 2, depth, channels), BF16)],
+        (18 * sides + 3 * size_y) * line_flops,
+        12,
+    )
+    skipped_three, out_two, *mores = call(
+        functools.partial(kernel_b1, **static),
+        [far_one, *far_halos, part_one, part_two, *border, out_two, out_three, first_weight, second_weight],
+        [(plane_shape, BF16), (plane_shape, F32), ((inner, depth, channels), F32)] + [(border_shape, F32)] * sides,
+        [field_of_plane, layer_of_plane],
+        4 * size_y * line_flops,
+        12,
+    )
+    skipped_two, pooled = call(
+        functools.partial(kernel_b2, **static),
+        [far_zero, *far_halos, skipped_three, out_two, *mores, first_weight, second_weight],
+        [(plane_shape, BF16), ((size_y // 2, depth // 2, channels), BF16)],
+        [field_of_plane, layer_of_plane, pltpu.VMEM((channels // LANES, size_y, depth, LANES), F32)],
+        2 * size_y * line_flops,
+        12,
     )
 
     turns = [(lambda c, step=step: (c + step) % chans) for step in range(chans)]
     own_blocks = [pooled] + [exchange(pooled, "own", turn) for turn in turns[1:]]
-    far_blocks = [exchange(pooled, "far")]
-    far_blocks += [exchange(block, "far") for block in own_blocks[1:]]
+    far_blocks = [exchange(pooled, "far", turn) for turn in turns[1:]]
+    far_blocks = [exchange(pooled, "far")] + far_blocks
     near_blocks = [exchange(pooled, "near")]
     near_blocks += [exchange(block, "near") for block in own_blocks[1:]]
     part_shape = (size_y // 2, depth // 2, channels)
@@ -342,7 +407,7 @@
     received = [exchange(part, "own", turn) for part, turn in zip(parts[1:], turns[1:])]
     return call(
         kernel_d,
-        [skipped, parts[0], *received],
+        [skipped_two, skipped_three, parts[0], *received],
         [(volume.shape, BF16)],
         [pltpu.VMEM((channels // LANES, size_y // 2, depth, LANES), F32)],
         volume.size,

time: 43.7 us -> 39.3 us (0.90)
  starting transfers between devices: 19.2 us -> 13.8 us
  Pallas kernels: 15 us -> 15.5 us
    ppermute x11 -> x12, starting transfers between devices: 19.2 us -> 13.8 us  [exchange(): return lax.ppermute(value, AXES, pairs)]
    pallas_call x6 -> x8, Pallas kernels: 15 us -> 15.5 us  [call(): pl.pallas_call(kernel, out_shape=out_shape, in_specs=[VMEM_SPEC] * len(in...]
    ppermute x11 -> x12, waiting for transfers between devices: 8.74 us -> 9.14 us  [exchange(): return lax.ppermute(value, AXES, pairs)]
  transfers between devices with their start and end apart: 11 -> 12, of which waited for: 4 -> 4; matrix products, arithmetic and copies ran while one was open for 0% -> 0% of each run, Pallas kernels for 19% -> 29%
where the time goes in v1:
time: 39.3 us; the launch traced here: 39.1 us
  Pallas kernels  15.5 us (39%)
  starting transfers between devices  13.8 us (35%)
  waiting for transfers between devices  9.14 us (23%)
  local copies, waits for them, and re-layouts  0.57 us (1%)
    pallas_call x8, Pallas kernels, call(): pl.pallas_call(kernel, out_shape=out_shape, in_specs=[VMEM_SPEC] * len(in...  15.5 us
    ppermute x12, starting transfers between devices, exchange(): return lax.ppermute(value, AXES, pairs)  13.8 us
    ppermute x12, waiting for transfers between devices, exchange(): return lax.ppermute(value, AXES, pairs)  9.14 us
  transfers between devices with their start and end apart: 12, of which 4 were waited for; matrix products, arithmetic and copies ran while one was open for 0% of the time, Pallas kernels for 29%

profile of v1, /device:TPU:0, one launch (start us, length us, event | category | flops | bytes accessed | tf_op | source)
XLA Modules:
  0.0 39.1 jit_solution(7235489526400715026)
XLA Ops:
  0.0 0.5 %collective-permute-start.4 = (bf16[2,8,64,256]{3,2,1,0:T(8,128)(2,1)}, bf16[2,8,64,256]{3,2,1,0:T(8,128)(2,1)S(1)}, u32[]{:S(2)}, u32[]{:S(2)}) collective-permute-start(bf16[2,8,64,256]{3,2,1,0:T(8,128)(2,1)} %refs_0_.1), channel_id=1, source_target_pairs={{0,2},{1,3},{2,0},{3,1},{4,6},{5,7},{6,4},{7,5},{8,10},{9,11},{10,... | collective-permute-start | bytes 1572872 | tf_op jit(solution)/shard_map/ppermute | solution.py:37
  0.5 0.5 %copy-done.4 = bf16[2,8,64,256]{3,2,1,0:T(8,128)(2,1)S(1)} copy-done((bf16[2,8,64,256]{3,2,1,0:T(8,128)(2,1)S(1)}, bf16[2,8,64,256]{3,2,1,0:T(8,128)(2,1)}, u32[]{:S(2)}) %copy-start.4) | copy-done | bytes 524312
  1.1 3.0 %collective-permute-start.1 = (bf16[2,2,64,256]{3,2,1,0:T(8,128)(2,1)S(1)}, bf16[2,2,64,256]{3,2,1,0:T(8,128)(2,1)S(1)}, u32[]{:S(2)}, u32[]{:S(2)}) collective-permute-start(bf16[2,2,64,256]{3,2,1,0:T(8,128)(2,1)S(1)} %get-tuple-element.25), channel_id=1, source_target_pairs={{0,1},{1,0},{2,3},{3,2},{4,5},{5,4},{6,7},{7,6},{8,9},{9,8},{10,11... | collective-permute-start | bytes 393224 | tf_op jit(solution)/shard_map/ppermute | solution.py:37
  4.1 0.1 collective-permute-start
  4.2 1.9 %collective-permute-start.3 = (bf16[8,64,256]{2,1,0:T(8,128)(2,1)S(1)}, bf16[8,64,256]{2,1,0:T(8,128)(2,1)S(1)}, u32[]{:S(2)}, u32[]{:S(2)}) collective-permute-start(bf16[8,64,256]{2,1,0:T(8,128)(2,1)S(1)} %get-tuple-element.26), channel_id=1, source_target_pairs={{0,1},{1,0},{2,4},{3,5},{4,2},{5,3},{6,8},{7,9},{8,6},{9,7},{10,12... | collective-permute-start | bytes 786440 | tf_op jit(solution)/shard_map/ppermute | solution.py:37
  6.2 1.5 %collective-permute-done.1.refs_1_ = bf16[2,2,64,256]{3,2,1,0:T(8,128)(2,1)S(1)} collective-permute-done((bf16[2,2,64,256]{3,2,1,0:T(8,128)(2,1)S(1)}, bf16[2,2,64,256]{3,2,1,0:T(8,128)(2,1)S(1)}, u32[]{:S(2)}, u32[]{:S(2)}) %collective-permute-start.1) | collective-permute-done | bytes 131104 | tf_op jit(solution)/shard_map/ppermute | solution.py:37
  7.6 0.0 collective-permute-start.5
  7.6 1.7 %collective-permute-start.2 = (bf16[2,2,64,256]{3,2,1,0:T(8,128)(2,1)S(1)}, bf16[2,2,64,256]{3,2,1,0:T(8,128)(2,1)S(1)}, u32[]{:S(2)}, u32[]{:S(2)}) collective-permute-start(bf16[2,2,64,256]{3,2,1,0:T(8,128)(2,1)S(1)} %collective-permute-done.1.refs_1_), channel_id=1, source_target_pairs={{0,1},{1,0},{2,4},{3,5},{4,2},{5,3},{6,8},{7,9},{8,6},{9,7},{10,12... | collective-permute-start | bytes 393224 | tf_op jit(solution)/shard_map/ppermute | solution.py:37
  9.4 0.0 collective-permute-done.4.near.refs_2_
  9.4 5.0 %shard_map.57 = (bf16[7,64,256]{2,1,0:T(8,128)(2,1)S(1)}, bf16[7,64,256]{2,1,0:T(8,128)(2,1)S(1)}, f32[7,64,256]{2,1,0:T(8,128)S(1)}, f32[7,64,256]{2,1,0:T(8,128)S(1)}) custom-call(bf16[2,8,64,256]{3,2,1,0:T(8,128)(2,1)S(1)} %copy-done.4, bf16[2,8,64,256]{3,2,1,0:T(8,128)(2,1)S(1)} %collective-permute-done.4.near.refs_2_, ...), custom_call_target="tpu_custom_call" | custom-call | flops 4756340736 | bytes 1048576 | tf_op jit(solution)/shard_map/pallas_call | solution.py:66
  14.4 0.0 collective-permute-done.5.refs_3_
  14.4 3.4 %shard_map.58 = (f32[8,64,256]{2,1,0:T(8,128)S(1)}, f32[8,64,256]{2,1,0:T(8,128)S(1)}, f32[2,64,256]{2,1,0:T(8,128)S(1)}, f32[2,64,256]{2,1,0:T(8,128)S(1)}) custom-call(bf16[2,8,64,256]{3,2,1,0:T(8,128)(2,1)S(1)} %copy-done.4, bf16[2,2,64,256]{3,2,1,0:T(8,128)(2,1)S(1)} %collective-permute-done.1.refs_1_, ...), custom_call_target="tpu_custom_call" | custom-call | flops 3170893824 | bytes 1048576 | tf_op jit(solution)/shard_map/pallas_call | solution.py:66
  17.9 0.0 collective-permute-done.2.refs_1_
  17.9 0.0 collective-permute-done.3.refs_0_
  17.9 2.9 %shard_map.59 = (bf16[8,64,256]{2,1,0:T(8,128)(2,1)S(1)}, f32[8,64,256]{2,1,0:T(8,128)S(1)}, f32[7,64,256]{2,1,0:T(8,128)S(1)}, f32[2,64,256]{2,1,0:T(8,128)S(1)}) custom-call(bf16[8,64,256]{2,1,0:T(8,128)(2,1)S(1)} %collective-permute-done.3.refs_0_, bf16[2,2,64,256]{3,2,1,0:T(8,128)(2,1)S(1)} %collective-permute-done.2.refs_1_, ...), custom_call_target="tpu_custom_call" | custom-call | flops 2415919104 | bytes 1048576 | tf_op jit(solution)/shard_map/pallas_call | solution.py:66
  20.8 0.0 collective-permute-done.refs_0_
  20.8 0.0 copy-start.2
  20.8 0.0 copy-start.3
  20.8 1.9 %shard_map.60 = (bf16[8,64,256]{2,1,0:T(8,128)(2,1)S(1)}, bf16[4,32,256]{2,1,0:T(8,128)(2,1)S(1)}) custom-call(bf16[8,64,256]{2,1,0:T(8,128)(2,1)S(1)} %collective-permute-done.refs_0_, bf16[2,2,64,256]{3,2,1,0:T(8,128)(2,1)S(1)} %collective-permute-done.2.refs_1_, bf16[8,64,256]{2,1,0:T(8,128)(2,1)S(1)} %get-tuple-element.35.refs_2_.refs_1_, ...), custom_call_target="tpu_custom_call" | custom-call | flops 1207959552 | bytes 1048576 | tf_op jit(solution)/shard_map/pallas_call | solution.py:66
  22.7 0.3 collective-permute-start.8
  23.1 2.4 %collective-permute-start.9 = (bf16[4,32,256]{2,1,0:T(8,128)(2,1)S(1)}, bf16[4,32,256]{2,1,0:T(8,128)(2,1)S(1)}, u32[]{:S(2)}, u32[]{:S(2)}) collective-permute-start(bf16[4,32,256]{2,1,0:T(8,128)(2,1)S(1)} %get-tuple-element.40.refs_2_), channel_id=1, source_target_pairs={{0,2},{1,3},{2,0},{3,1},{4,6},{5,7},{6,4},{7,5},{8,10},{9,11},{10,... | collective-permute-start | bytes 196616 | tf_op jit(solution)/shard_map/ppermute | solution.py:37
  25.5 1.5 %collective-permute-start.7 = (bf16[4,32,256]{2,1,0:T(8,128)(2,1)S(1)}, bf16[4,32,256]{2,1,0:T(8,128)(2,1)S(1)}, u32[]{:S(2)}, u32[]{:S(2)}) collective-permute-start(bf16[4,32,256]{2,1,0:T(8,128)(2,1)S(1)} %get-tuple-element.40.refs_2_), channel_id=1, source_target_pairs={{0,1},{1,0},{2,5},{3,4},{4,3},{5,2},{6,9},{7,8},{8,7},{9,6},{10,13... | collective-permute-start | bytes 196616 | tf_op jit(solution)/shard_map/ppermute | solution.py:37
  27.0 0.5 %collective-permute-start.6 = (bf16[4,32,256]{2,1,0:T(8,128)(2,1)S(1)}, bf16[4,32,256]{2,1,0:T(8,128)(2,1)S(1)}, u32[]{:S(2)}, u32[]{:S(2)}) collective-permute-start(bf16[4,32,256]{2,1,0:T(8,128)(2,1)S(1)} %get-tuple-element.40.refs_2_), channel_id=1, source_target_pairs={{0,1},{1,0},{2,4},{3,5},{4,2},{5,3},{6,8},{7,9},{8,6},{9,7},{10,12... | collective-permute-start | bytes 196616 | tf_op jit(solution)/shard_map/ppermute | solution.py:37
  27.5 0.0 collective-permute-done.8.refs_3_
  27.5 1.7 %collective-permute-start.10 = (bf16[4,32,256]{2,1,0:T(8,128)(2,1)S(1)}, bf16[4,32,256]{2,1,0:T(8,128)(2,1)S(1)}, u32[]{:S(2)}, u32[]{:S(2)}) collective-permute-start(bf16[4,32,256]{2,1,0:T(8,128)(2,1)S(1)} %collective-permute-done.8.refs_3_), channel_id=1, source_target_pairs={{0,2},{1,3},{2,0},{3,1},{4,6},{5,7},{6,4},{7,5},{8,10},{9,11},{10,... | collective-permute-start | bytes 196616 | tf_op jit(solution)/shard_map/ppermute | solution.py:37
  29.2 0.0 collective-permute-done.9.refs_4_
  29.2 0.6 %collective-permute-done.7.refs_1_ = bf16[4,32,256]{2,1,0:T(8,128)(2,1)S(1)} collective-permute-done((bf16[4,32,256]{2,1,0:T(8,128)(2,1)S(1)}, bf16[4,32,256]{2,1,0:T(8,128)(2,1)S(1)}, u32[]{:S(2)}, u32[]{:S(2)}) %collective-permute-start.7) | collective-permute-done | bytes 65568 | tf_op jit(solution)/shard_map/ppermute | solution.py:37
  29.7 2.2 %collective-permute-done.6.refs_0_ = bf16[4,32,256]{2,1,0:T(8,128)(2,1)S(1)} collective-permute-done((bf16[4,32,256]{2,1,0:T(8,128)(2,1)S(1)}, bf16[4,32,256]{2,1,0:T(8,128)(2,1)S(1)}, u32[]{:S(2)}, u32[]{:S(2)}) %collective-permute-start.6) | collective-permute-done | bytes 65568 | tf_op jit(solution)/shard_map/ppermute | solution.py:37
  31.9 1.3 %shard_map.61 = (f32[4,32,256]{2,1,0:T(8,128)S(1)}, bf16[4,32,256]{2,1,0:T(8,128)(2,1)S(1)}) custom-call(bf16[4,32,256]{2,1,0:T(8,128)(2,1)S(1)} %collective-permute-done.6.refs_0_, bf16[4,32,256]{2,1,0:T(8,128)(2,1)S(1)} %collective-permute-done.7.refs_1_, bf16[4,32,256]{2,1,0:T(8,128)(2,1)S(1)} %get-tuple-element.40.refs_2_, ...), custom_call_target="tpu_custom_call" | custom-call | flops 905969664 | bytes 1048576 | tf_op jit(solution)/shard_map/pallas_call | solution.py:66
  33.2 0.1 collective-permute-start.11
  33.3 4.9 %collective-permute-done.11.refs_3_ = bf16[4,32,256]{2,1,0:T(8,128)(2,1)S(1)} collective-permute-done((bf16[4,32,256]{2,1,0:T(8,128)(2,1)S(1)}, bf16[4,32,256]{2,1,0:T(8,128)(2,1)S(1)}, u32[]{:S(2)}, u32[]{:S(2)}) %collective-permute-start.11) | collective-permute-done | bytes 65568 | tf_op jit(solution)/shard_map/ppermute | solution.py:37
  38.2 0.9 %shard_map.62 = bf16[2,8,64,256]{3,2,1,0:T(8,128)(2,1)} custom-call(bf16[8,64,256]{2,1,0:T(8,128)(2,1)S(1)} %get-tuple-element.39.refs_0_, bf16[8,64,256]{2,1,0:T(8,128)(2,1)S(1)} %get-tuple-element.35.refs_2_.refs_1_, f32[4,32,256]{2,1,0:T(8,128)S(1)} %get-tuple-element.41.refs_2_, bf16[4,32,256]{2,1,0:T(8,128)(2,1)S(1)} %collective-permute-done.11.refs_3_), custom_call_target="tpu_custom_call" | custom-call | flops 262144 | bytes 1048576 | tf_op jit(solution)/shard_map/pallas_call | solution.py:66
  (10 shorter events, 0.1 us)
Async XLA Ops:
  0.0 1.0 %copy-start.4 = (bf16[2,8,64,256]{3,2,1,0:T(8,128)(2,1)S(1)}, bf16[2,8,64,256]{3,2,1,0:T(8,128)(2,1)}, u32[]{:S(2)}) copy-start(bf16[2,8,64,256]{3,2,1,0:T(8,128)(2,1)} %refs_0_.1) | copy-start | bytes 1572868
  0.0 9.4 %collective-permute-start.4 = (bf16[2,8,64,256]{3,2,1,0:T(8,128)(2,1)}, bf16[2,8,64,256]{3,2,1,0:T(8,128)(2,1)S(1)}, u32[]{:S(2)}, u32[]{:S(2)}) collective-permute-start(bf16[2,8,64,256]{3,2,1,0:T(8,128)(2,1)} %refs_0_.1), channel_id=1, source_target_pairs={{0,2},{1,3},{2,0},{3,1},{4,6},{5,7},{6,4},{7,5},{8,10},{9,11},{10,... | collective-permute-start | bytes 1572872 | tf_op jit(solution)/shard_map/ppermute | solution.py:37
  1.0 8.3 %copy-start = (bf16[3,3,3,256,256]{4,3,2,1,0:T(8,128)(2,1)S(1)}, bf16[3,3,3,256,256]{4,3,2,1,0:T(8,128)(2,1)}, u32[]{:S(2)}) copy-start(bf16[3,3,3,256,256]{4,3,2,1,0:T(8,128)(2,1)} %refs_6_.4) | copy-start | bytes 10616836
  1.1 6.5 %collective-permute-start.1 = (bf16[2,2,64,256]{3,2,1,0:T(8,128)(2,1)S(1)}, bf16[2,2,64,256]{3,2,1,0:T(8,128)(2,1)S(1)}, u32[]{:S(2)}, u32[]{:S(2)}) collective-permute-start(bf16[2,2,64,256]{3,2,1,0:T(8,128)(2,1)S(1)} %get-tuple-element.25), channel_id=1, source_target_pairs={{0,1},{1,0},{2,3},{3,2},{4,5},{5,4},{6,7},{7,6},{8,9},{9,8},{10,11... | collective-permute-start | bytes 393224 | tf_op jit(solution)/shard_map/ppermute | solution.py:37
  4.1 16.6 %collective-permute-start = (bf16[8,64,256]{2,1,0:T(8,128)(2,1)S(1)}, bf16[8,64,256]{2,1,0:T(8,128)(2,1)S(1)}, u32[]{:S(2)}, u32[]{:S(2)}) collective-permute-start(bf16[8,64,256]{2,1,0:T(8,128)(2,1)S(1)} %get-tuple-element.24), channel_id=1, source_target_pairs={{0,1},{1,0},{2,4},{3,5},{4,2},{5,3},{6,8},{7,9},{8,6},{9,7},{10,12... | collective-permute-start | bytes 786440 | tf_op jit(solution)/shard_map/ppermute | solution.py:37
  4.2 10.2 %copy-start.1 = (bf16[3,3,3,256,256]{4,3,2,1,0:T(8,128)(2,1)S(1)}, bf16[3,3,3,256,256]{4,3,2,1,0:T(8,128)(2,1)}, u32[]{:S(2)}) copy-start(bf16[3,3,3,256,256]{4,3,2,1,0:T(8,128)(2,1)} %refs_7_.4) | copy-start | bytes 10616836
  4.2 13.7 %collective-permute-start.3 = (bf16[8,64,256]{2,1,0:T(8,128)(2,1)S(1)}, bf16[8,64,256]{2,1,0:T(8,128)(2,1)S(1)}, u32[]{:S(2)}, u32[]{:S(2)}) collective-permute-start(bf16[8,64,256]{2,1,0:T(8,128)(2,1)S(1)} %get-tuple-element.26), channel_id=1, source_target_pairs={{0,1},{1,0},{2,4},{3,5},{4,2},{5,3},{6,8},{7,9},{8,6},{9,7},{10,12... | collective-permute-start | bytes 786440 | tf_op jit(solution)/shard_map/ppermute | solution.py:37
  7.6 6.8 %collective-permute-start.5 = (bf16[2,2,64,256]{3,2,1,0:T(8,128)(2,1)S(1)}, bf16[2,2,64,256]{3,2,1,0:T(8,128)(2,1)S(1)}, u32[]{:S(2)}, u32[]{:S(2)}) collective-permute-start(bf16[2,2,64,256]{3,2,1,0:T(8,128)(2,1)S(1)} %collective-permute-done.1.refs_1_), channel_id=1, source_target_pairs={{0,2},{1,3},{2,0},{3,1},{4,6},{5,7},{6,4},{7,5},{8,10},{9,11},{10,... | collective-permute-start | bytes 393224 | tf_op jit(solution)/shard_map/ppermute | solution.py:37
  7.6 10.2 %collective-permute-start.2 = (bf16[2,2,64,256]{3,2,1,0:T(8,128)(2,1)S(1)}, bf16[2,2,64,256]{3,2,1,0:T(8,128)(2,1)S(1)}, u32[]{:S(2)}, u32[]{:S(2)}) collective-permute-start(bf16[2,2,64,256]{3,2,1,0:T(8,128)(2,1)S(1)} %collective-permute-done.1.refs_1_), channel_id=1, source_target_pairs={{0,1},{1,0},{2,4},{3,5},{4,2},{5,3},{6,8},{7,9},{8,6},{9,7},{10,12... | collective-permute-start | bytes 393224 | tf_op jit(solution)/shard_map/ppermute | solution.py:37
  20.8 11.1 %copy-start.2 = (bf16[3,3,3,256,256]{4,3,2,1,0:T(8,128)(2,1)S(1)}, bf16[3,3,3,256,256]{4,3,2,1,0:T(8,128)(2,1)}, u32[]{:S(2)}) copy-start(bf16[3,3,3,256,256]{4,3,2,1,0:T(8,128)(2,1)} %refs_6_.5) | copy-start | bytes 10616836
  20.8 11.1 %copy-start.3 = (bf16[256,256]{1,0:T(8,128)(2,1)S(1)}, bf16[256,256]{1,0:T(8,128)(2,1)}, u32[]{:S(2)}) copy-start(bf16[256,256]{1,0:T(8,128)(2,1)} %refs_7_.5) | copy-start | bytes 393220
  22.7 4.8 %collective-permute-start.8 = (bf16[4,32,256]{2,1,0:T(8,128)(2,1)S(1)}, bf16[4,32,256]{2,1,0:T(8,128)(2,1)S(1)}, u32[]{:S(2)}, u32[]{:S(2)}) collective-permute-start(bf16[4,32,256]{2,1,0:T(8,128)(2,1)S(1)} %get-tuple-element.40.refs_2_), channel_id=1, source_target_pairs={{0,1},{1,0},{2,3},{3,2},{4,5},{5,4},{6,7},{7,6},{8,9},{9,8},{10,11... | collective-permute-start | bytes 196616 | tf_op jit(solution)/shard_map/ppermute | solution.py:37
  23.1 6.1 %collective-permute-start.9 = (bf16[4,32,256]{2,1,0:T(8,128)(2,1)S(1)}, bf16[4,32,256]{2,1,0:T(8,128)(2,1)S(1)}, u32[]{:S(2)}, u32[]{:S(2)}) collective-permute-start(bf16[4,32,256]{2,1,0:T(8,128)(2,1)S(1)} %get-tuple-element.40.refs_2_), channel_id=1, source_target_pairs={{0,2},{1,3},{2,0},{3,1},{4,6},{5,7},{6,4},{7,5},{8,10},{9,11},{10,... | collective-permute-start | bytes 196616 | tf_op jit(solution)/shard_map/ppermute | solution.py:37
  25.5 4.3 %collective-permute-start.7 = (bf16[4,32,256]{2,1,0:T(8,128)(2,1)S(1)}, bf16[4,32,256]{2,1,0:T(8,128)(2,1)S(1)}, u32[]{:S(2)}, u32[]{:S(2)}) collective-permute-start(bf16[4,32,256]{2,1,0:T(8,128)(2,1)S(1)} %get-tuple-element.40.refs_2_), channel_id=1, source_target_pairs={{0,1},{1,0},{2,5},{3,4},{4,3},{5,2},{6,9},{7,8},{8,7},{9,6},{10,13... | collective-permute-start | bytes 196616 | tf_op jit(solution)/shard_map/ppermute | solution.py:37
  27.0 4.9 %collective-permute-start.6 = (bf16[4,32,256]{2,1,0:T(8,128)(2,1)S(1)}, bf16[4,32,256]{2,1,0:T(8,128)(2,1)S(1)}, u32[]{:S(2)}, u32[]{:S(2)}) collective-permute-start(bf16[4,32,256]{2,1,0:T(8,128)(2,1)S(1)} %get-tuple-element.40.refs_2_), channel_id=1, source_target_pairs={{0,1},{1,0},{2,4},{3,5},{4,2},{5,3},{6,8},{7,9},{8,6},{9,7},{10,12... | collective-permute-start | bytes 196616 | tf_op jit(solution)/shard_map/ppermute | solution.py:37
  27.5 4.4 %collective-permute-start.10 = (bf16[4,32,256]{2,1,0:T(8,128)(2,1)S(1)}, bf16[4,32,256]{2,1,0:T(8,128)(2,1)S(1)}, u32[]{:S(2)}, u32[]{:S(2)}) collective-permute-start(bf16[4,32,256]{2,1,0:T(8,128)(2,1)S(1)} %collective-permute-done.8.refs_3_), channel_id=1, source_target_pairs={{0,2},{1,3},{2,0},{3,1},{4,6},{5,7},{6,4},{7,5},{8,10},{9,11},{10,... | collective-permute-start | bytes 196616 | tf_op jit(solution)/shard_map/ppermute | solution.py:37
  33.2 5.0 %collective-permute-start.11 = (bf16[4,32,256]{2,1,0:T(8,128)(2,1)S(1)}, bf16[4,32,256]{2,1,0:T(8,128)(2,1)S(1)}, u32[]{:S(2)}, u32[]{:S(2)}) collective-permute-start(bf16[4,32,256]{2,1,0:T(8,128)(2,1)S(1)} %get-tuple-element.42), channel_id=1, source_target_pairs={{0,1},{1,0},{2,3},{3,2},{4,5},{5,4},{6,7},{7,6},{8,9},{9,8},{10,11... | collective-permute-start | bytes 196616 | tf_op jit(solution)/shard_map/ppermute | solution.py:37

commit v2 on v1

--- a/solution.py
+++ b/solution.py
@@ -101,15 +101,6 @@
     return step + odd * (2 - 2 * step)
 
 
-def halo_plan(chans, size_y):
-    chan = lax.axis_index("chan")
-    if chans == 1:
-        return []
-    if chans == 2:
-        return [(jnp.where(chan == 1, 0, size_y + 2), jnp.where(chan == 1, size_y + 2, 0))]
-    return [(0, None), (size_y + 2, None)]
-
-
 def inner_rows(chans, size_y):
     return {1: (0, size_y), 2: (lax.axis_index("chan"), size_y - 1)}.get(chans, (1, size_y - 2))
 
@@ -122,26 +113,27 @@
     return [(-1, 2), (size_y - 1, 2)]
 
 
-def row_groups(chans, size_y):
-    return [inner_rows(chans, size_y), *border_rows(chans, size_y)]
-
-
-def fill_plane(target, block, plane, halos, chans):
-    valid = has_far()
-
-    def masked(rows):
-        return jnp.where(valid, rows, jnp.zeros_like(rows))
-
-    size_y = block.shape[0]
-    target[0, 2 : size_y + 2] = masked(block[...])
-    zeros = jnp.zeros((2,) + target.shape[2:], target.dtype)
-    if chans == 1:
-        target[0, 0:2] = zeros
-        target[0, size_y + 2 : size_y + 4] = zeros
-    for (place, empty), halo in zip(halo_plan(chans, size_y), halos):
-        target[0, pl.ds(place, 2)] = masked(halo[plane])
-        if empty is not None:
-            target[0, pl.ds(empty, 2)] = zeros
+def fill_inner(target, planes, valid=None):
+    size_y = target.shape[1] - 2
+    zeros = jnp.zeros(target.shape[2:], target.dtype)
+    for slot, (block, plane) in enumerate(planes):
+        rows = block[...] if plane is None else block[plane]
+        target[slot, 0] = zeros
+        target[slot, 1 : size_y + 1] = rows if valid is None else jnp.where(valid, rows, jnp.zeros_like(rows))
+        target[slot, size_y + 1] = zeros
+
+
+def fill_border(target, start, size_y, planes, valid=None):
+    high = start > 0
+    place, source = jnp.where(high, 0, 2), jnp.where(high, size_y - 2, 0)
+    for slot, (block, plane, halo, halo_plane) in enumerate(planes):
+        rows = block[pl.ds(source, 2)] if plane is None else block[plane, pl.ds(source, 2)]
+        beyond = halo[halo_plane]
+        if valid is not None:
+            rows = jnp.where(valid, rows, jnp.zeros_like(rows))
+            beyond = jnp.where(valid, beyond, jnp.zeros_like(beyond))
+        target[slot, pl.ds(place, 2)] = rows
+        target[slot, pl.ds(2 - place, 2)] = beyond
 
 
 def clear_outside(layer, slot, chans):
@@ -158,11 +150,7 @@
 def kernel_a0(own, near, weight_one, done_three, done_four, part_one, part_two, field, *, chans):
     odd = lax.rem(lax.axis_index("brick"), 2)
     size_y = own.shape[1]
-    zeros = jnp.zeros(field.shape[2:], field.dtype)
-    for slot, (block, plane) in enumerate(((own, odd), (own, 1 - odd), (near, odd), (near, 1 - odd))):
-        field[slot, 0] = zeros
-        field[slot, 1 : size_y + 1] = block[plane]
-        field[slot, size_y + 1] = zeros
+    fill_inner(field, ((own, odd), (own, 1 - odd), (near, odd), (near, 1 - odd)))
     first, rows = inner_rows(chans, size_y)
     lines = tile_of(rows)
     for row in range(0, rows, lines):
@@ -188,12 +176,9 @@
     layer[0, pl.ds(first + 1, rows)] = done_three[...]
     layer[1, pl.ds(first + 1, rows)] = done_four[...]
     for side, (start, count) in enumerate(border_rows(chans, size_y)):
-        high = start > 0
-        place, source = jnp.where(high, 0, 2), jnp.where(high, size_y - 2, 0)
-        planes = ((own, own_halos, odd), (own, own_halos, 1 - odd), (near, near_halos, odd), (near, near_halos, 1 - odd))
-        for slot, (block, halos, plane) in enumerate(planes):
-            field[slot, pl.ds(place, 2)] = block[plane, pl.ds(source, 2)]
-            field[slot, pl.ds(2 - place, 2)] = halos[side][plane]
+        pairs = ((own, own_halos[side], odd), (own, own_halos[side], 1 - odd))
+        pairs += ((near, near_halos[side], odd), (near, near_halos[side], 1 - odd))
+        fill_border(field, start, size_y, [(block, plane, halo, plane) for block, halo, plane in pairs])
         for slot in range(2):
             terms = [(field, slot + step, tap(step, odd)) for step in range(3)]
             value = jnp.maximum(conv_lines(terms, 0, count, weight_one), 0.0).astype(BF16)
@@ -210,55 +195,52 @@
         out_three[spot] = conv_lines([(layer, 0, tap(1, odd)), (layer, 1, tap(2, odd))], row, lines, weight_two)
 
 
+def kernel_b0(plane_one, plane_zero, part_one, part_two, weight_one, done_one, done_two, field, *, chans):
+    odd = lax.rem(lax.axis_index("brick"), 2)
+    valid = has_far()
+    fill_inner(field, ((plane_zero, None), (plane_one, None)), valid)
+    first, rows = inner_rows(chans, plane_one.shape[0])
+    lines = tile_of(rows)
+    for row in range(0, rows, lines):
+        spot, base = pl.ds(row, lines), first + row
+        value = conv_lines([(field, 0, tap(0, odd)), (field, 1, tap(1, odd))], base, lines, weight_one)
+        value = jnp.maximum(value + part_one[spot], 0.0)
+        done_one[spot] = jnp.where(valid, value, 0.0).astype(BF16)
+        value = conv_lines([(field, 1, tap(0, odd))], base, lines, weight_one)
+        done_two[spot] = jnp.maximum(value + part_two[spot], 0.0).astype(BF16)
+
+
 def kernel_b1(*refs, chans, sides):
-    block, halos, refs = refs[0], refs[1 : 1 + sides], refs[1 + sides :]
-    part_one, part_two, out_two, out_three, weight_one, weight_two = refs[0], refs[1], *refs[2 + 2 * sides : 6 + 2 * sides]
-    ones, twos = [part_one, *refs[2 : 2 + sides]], [part_two, *refs[2 + sides : 2 + 2 * sides]]
-    refs = refs[6 + 2 * sides :]
-    skipped, more_two, mores = refs[0], refs[1], refs[2 : 3 + sides]
-    field, layer = refs[3 + sides :]
-    odd = lax.rem(lax.axis_index("brick"), 2)
-    size_y = block.shape[0]
-    fill_plane(field, block, 1 - odd, halos, chans)
-    for (start, rows), one, two, more in zip(row_groups(chans, size_y), ones, twos, mores):
-        lines = tile_of(rows)
-        for row in range(0, rows, lines):
-            spot, base = pl.ds(row, lines), start + row + 1
-            value = conv_lines([(field, 0, tap(0, odd))], base, lines, weight_one)
-            layer[0, pl.ds(base, lines)] = jnp.maximum(value + two[spot], 0.0).astype(BF16)
-            more[spot] = one[spot] + conv_lines([(field, 0, tap(1, odd))], base, lines, weight_one)
-    clear_outside(layer, 0, chans)
+    plane_one, plane_zero, halos = refs[0], refs[1], refs[2 : 2 + sides]
+    done_one, done_two, out_two, out_three, weight_one, weight_two = refs[2 + sides : 8 + sides]
+    parts = refs[8 + sides : 8 + 3 * sides]
+    skipped_two, skipped_three, pooled, field, layer, sums = refs[8 + 3 * sides :]
+    odd = lax.rem(lax.axis_index("brick"), 2)
+    valid = has_far()
+    size_y, depth = plane_one.shape[0], plane_one.shape[1]
+    first, rows = inner_rows(chans, size_y)
+    layer[0, pl.ds(first + 1, rows)] = done_one[...]
+    layer[1, pl.ds(first + 1, rows)] = done_two[...]
+    for side, (start, count) in enumerate(border_rows(chans, size_y)):
+        planes = ((plane_zero, None, halos[side], odd), (plane_one, None, halos[side], 1 - odd))
+        fill_border(field, start, size_y, planes, valid)
+        value = conv_lines([(field, 0, tap(0, odd)), (field, 1, tap(1, odd))], 0, count, weight_one)
+        value = jnp.maximum(value + parts[side][...], 0.0)
+        layer[0, pl.ds(start + 1, count)] = jnp.where(valid, value, 0.0).astype(BF16)
+        value = conv_lines([(field, 1, tap(0, odd))], 0, count, weight_one)
+        layer[1, pl.ds(start + 1, count)] = jnp.maximum(value + parts[sides + side][...], 0.0).astype(BF16)
+    for slot in range(2):
+        clear_outside(layer, slot, chans)
     lines = tile_of(size_y)
     for row in range(0, size_y, lines):
         spot = pl.ds(row, lines)
-        value = conv_lines([(layer, 0, tap(0, odd))], row, lines, weight_two)
-        skipped[spot] = jnp.maximum(value + out_three[spot], 0.0).astype(BF16)
-        more_two[spot] = out_two[spot] + conv_lines([(layer, 0, tap(1, odd))], row, lines, weight_two)
-
-
-def kernel_b2(*refs, chans, sides):
-    block, halos, refs = refs[0], refs[1 : 1 + sides], refs[1 + sides :]
-    other, out_two, mores, weight_one, weight_two = refs[0], refs[1], refs[2 : 3 + sides], *refs[3 + sides : 5 + sides]
-    skipped, pooled, field, layer, sums = refs[5 + sides :]
-    odd = lax.rem(lax.axis_index("brick"), 2)
-    inside = has_far()
-    size_y, depth = block.shape[0], block.shape[1]
-    fill_plane(field, block, odd, halos, chans)
-    for (start, rows), more in zip(row_groups(chans, size_y), mores):
-        lines = tile_of(rows)
-        for row in range(0, rows, lines):
-            base = start + row + 1
-            value = conv_lines([(field, 0, tap(0, odd))], base, lines, weight_one)
-            value = jnp.maximum(value + more[pl.ds(row, lines)], 0.0)
-            layer[0, pl.ds(base, lines)] = jnp.where(inside, value, 0.0).astype(BF16)
-    clear_outside(layer, 0, chans)
-    lines = tile_of(size_y)
-    for row in range(0, size_y, lines):
-        spot = pl.ds(row, lines)
-        value = conv_lines([(layer, 0, tap(0, odd))], row, lines, weight_two)
-        value = jnp.maximum(value + out_two[spot], 0.0).astype(BF16)
-        skipped[spot] = value
-        both = value.astype(F32) + other[spot].astype(F32)
+        value = conv_lines([(layer, 0, tap(0, odd)), (layer, 1, tap(1, odd))], row, lines, weight_two)
+        two = jnp.maximum(value + out_two[spot], 0.0).astype(BF16)
+        skipped_two[spot] = two
+        value = conv_lines([(layer, 1, tap(0, odd))], row, lines, weight_two)
+        three = jnp.maximum(value + out_three[spot], 0.0).astype(BF16)
+        skipped_three[spot] = three
+        both = two.astype(F32) + three.astype(F32)
         for group in range(sums.shape[0]):
             sums[group, spot] = both[:, :, group * LANES : (group + 1) * LANES]
     for row in range(size_y // 2):
@@ -270,32 +252,45 @@
             pooled[row, :, group * LANES : (group + 1) * LANES] = mean.astype(BF16)
 
 
-def kernel_c(*refs, chans):
-    blocks = refs[: 3 * chans]
-    weight, projection = refs[3 * chans : 3 * chans + 2]
-    own_part, sent = refs[3 * chans + 2], refs[3 * chans + 3 : 4 * chans + 2]
-    field, parts = refs[4 * chans + 2 :]
+def fill_pooled(target, planes, valid=None):
+    chan, chans = lax.axis_index("chan"), len(planes[0])
+    zeros = jnp.zeros(target.shape[2:], target.dtype)
+    for slot, blocks in enumerate(planes):
+        rows = blocks[0].shape[0]
+        target[slot, 0] = zeros
+        target[slot, chans * rows + 1] = zeros
+        for step, block in enumerate(blocks):
+            source = lax.rem(chan - step + chans, chans)
+            value = block[...]
+            if valid is not None:
+                value = jnp.where(valid, value, jnp.zeros_like(value))
+            target[slot, pl.ds(1 + source * rows, rows)] = value
+
+
+def kernel_c1(*refs, chans):
+    weight, part, field = refs[2 * chans :]
+    odd = lax.rem(lax.axis_index("brick"), 2)
+    fill_pooled(field, (refs[:chans], refs[chans : 2 * chans]))
+    lines = tile_of(part.shape[0])
+    for row in range(0, part.shape[0], lines):
+        part[pl.ds(row, lines)] = conv_lines([(field, 0, tap(1, odd)), (field, 1, tap(2, odd))], row, lines, weight)
+
+
+def kernel_c2(*refs, chans):
+    part, weight, projection, own_part = refs[chans : chans + 4]
+    sent = refs[chans + 4 : 2 * chans + 3]
+    field, parts = refs[2 * chans + 3 :]
     odd = lax.rem(lax.axis_index("brick"), 2)
     chan = lax.axis_index("chan")
-    rows, depth = blocks[0].shape[0], blocks[0].shape[1]
-    total = chans * rows
-    inside = has_far()
-    for plane in range(3):
-        zeros = jnp.zeros(field.shape[2:], field.dtype)
-        field[plane, 0] = zeros
-        field[plane, total + 1] = zeros
-        for step in range(chans):
-            source = lax.rem(chan - step + chans, chans)
-            block = blocks[plane * chans + step][...]
-            if plane == 0:
-                block = jnp.where(inside, block, jnp.zeros_like(block))
-            field[plane, pl.ds(1 + source * rows, rows)] = block
+    total, depth = part.shape[0], part.shape[1]
+    rows = total // chans
+    fill_pooled(field, (refs[:chans],), has_far())
     lines = tile_of(total)
     for row in range(0, total, lines):
-        value = conv_lines([(field, step, tap(step, odd)) for step in range(3)], row, lines, weight)
+        value = conv_lines([(field, 0, tap(0, odd))], row, lines, weight) + part[pl.ds(row, lines)]
         value = jnp.maximum(value, 0.0).astype(BF16).reshape(lines * depth, weight.shape[4])
-        part = jnp.dot(value, projection[...], preferred_element_type=F32)
-        parts[pl.ds(row, lines)] = part.reshape(lines, depth, part.shape[1])
+        lifted = jnp.dot(value, projection[...], preferred_element_type=F32)
+        parts[pl.ds(row, lines)] = lifted.reshape(lines, depth, lifted.shape[1])
     own_part[...] = parts[pl.ds(chan * rows, rows)]
     for step in range(1, chans):
         target = lax.rem(chan + step, chans)
@@ -350,8 +345,6 @@
     inner = inner_rows(chans, size_y)[1]
     border_shape = (2, depth, channels)
     line_flops = 2 * depth * 9 * channels * channels
-    field_of_plane = pltpu.VMEM((1, size_y + 4, depth, channels), BF16)
-    layer_of_plane = pltpu.VMEM((1, size_y + 2, depth, channels), BF16)
     done_three, done_four, part_one, part_two = call(
         functools.partial(kernel_a0, chans=chans),
         [volume, near, first_weight],
@@ -368,20 +361,24 @@
         (18 * sides + 3 * size_y) * line_flops,
         12,
     )
-    skipped_three, out_two, *mores = call(
+    done_one, done_two = call(
+        functools.partial(kernel_b0, chans=chans),
+        [far_one, far_zero, part_one, part_two, first_weight],
+        [((inner, depth, channels), BF16)] * 2,
+        [pltpu.VMEM((2, size_y + 2, depth, channels), BF16)],
+        3 * inner * line_flops,
+        12,
+    )
+    skipped_two, skipped_three, pooled = call(
         functools.partial(kernel_b1, **static),
-        [far_one, *far_halos, part_one, part_two, *border, out_two, out_three, first_weight, second_weight],
-        [(plane_shape, BF16), (plane_shape, F32), ((inner, depth, channels), F32)] + [(border_shape, F32)] * sides,
-        [field_of_plane, layer_of_plane],
-        4 * size_y * line_flops,
-        12,
-    )
-    skipped_two, pooled = call(
-        functools.partial(kernel_b2, **static),
-        [far_zero, *far_halos, skipped_three, out_two, *mores, first_weight, second_weight],
-        [(plane_shape, BF16), ((size_y // 2, depth // 2, channels), BF16)],
-        [field_of_plane, layer_of_plane, pltpu.VMEM((channels // LANES, size_y, depth, LANES), F32)],
-        2 * size_y * line_flops,
+        [far_one, far_zero, *far_halos, done_one, done_two, out_two, out_three, first_weight, second_weight, *border],
+        [(plane_shape, BF16)] * 2 + [((size_y // 2, depth // 2, channels), BF16)],
+        [
+            pltpu.VMEM((2, 4, depth, channels), BF16),
+            pltpu.VMEM((2, size_y + 2, depth, channels), BF16),
+            pltpu.VMEM((channels // LANES, size_y, depth, LANES), F32),
+        ],
+        (6 * sides + 3 * size_y) * line_flops,
         12,
     )
 
@@ -393,16 +390,24 @@
     near_blocks += [exchange(block, "near") for block in own_blocks[1:]]
     part_shape = (size_y // 2, depth // 2, channels)
     coarse_rows = chans * size_y // 2
+    coarse_channels = coarse_weight.shape[4]
+    plane_flops = 2 * coarse_rows * (depth // 2) * 9 * channels * coarse_channels
+    coarse_field = (coarse_rows + 2, depth // 2, channels)
+    coarse_part = call(
+        functools.partial(kernel_c1, chans=chans),
+        [*own_blocks, *near_blocks, coarse_weight],
+        [((coarse_rows, depth // 2, coarse_channels), F32)],
+        [pltpu.VMEM((2,) + coarse_field, BF16)],
+        2 * plane_flops,
+        12,
+    )[0]
     parts = call(
-        functools.partial(kernel_c, chans=chans),
-        [*far_blocks, *own_blocks, *near_blocks, coarse_weight, projection],
+        functools.partial(kernel_c2, chans=chans),
+        [*far_blocks, coarse_part, coarse_weight, projection],
         [(part_shape, F32)] + [(part_shape, BF16)] * (chans - 1),
-        [
-            pltpu.VMEM((3, coarse_rows + 2, depth // 2, channels), BF16),
-            pltpu.VMEM((coarse_rows, depth // 2, channels), F32),
-        ],
-        2 * coarse_rows * (depth // 2) * 27 * channels * coarse_weight.shape[4],
-        16,
+        [pltpu.VMEM((1,) + coarse_field, BF16), pltpu.VMEM((coarse_rows, depth // 2, channels), F32)],
+        plane_flops,
+        12,
     )
     received = [exchange(part, "own", turn) for part, turn in zip(parts[1:], turns[1:])]
     return call(

time: 39.3 us -> 39.6 us (level)
  the two profiles are of different devices: /device:TPU:0 before, /device:TPU:21 now
where the time goes in v2:
time: 39.6 us; the launch traced here: 38.8 us
  starting transfers between devices  16.6 us (42%)
  Pallas kernels  15.5 us (39%)
  waiting for transfers between devices  6.15 us (16%)
    ppermute x12, starting transfers between devices, exchange(): return lax.ppermute(value, AXES, pairs)  16.6 us
    pallas_call x9, Pallas kernels, call(): pl.pallas_call(kernel, out_shape=out_shape, in_specs=[VMEM_SPEC] * len(in...  15.5 us
    ppermute x12, waiting for transfers between devices, exchange(): return lax.ppermute(value, AXES, pairs)  6.15 us
  transfers between devices with their start and end apart: 12, of which 4 were waited for; matrix products, arithmetic and copies ran while one was open for 0% of the time, Pallas kernels for 29%

profile of v2, /device:TPU:21, one launch (start us, length us, event | category | flops | bytes accessed | tf_op | source)
XLA Modules:
  0.0 38.8 jit_solution(1385789089483592713)
XLA Ops:
  0.0 0.7 %collective-permute-start.4 = (bf16[2,8,64,256]{3,2,1,0:T(8,128)(2,1)}, bf16[2,8,64,256]{3,2,1,0:T(8,128)(2,1)S(1)}, u32[]{:S(2)}, u32[]{:S(2)}) collective-permute-start(bf16[2,8,64,256]{3,2,1,0:T(8,128)(2,1)} %refs_0_.1), channel_id=1, source_target_pairs={{0,2},{1,3},{2,0},{3,1},{4,6},{5,7},{6,4},{7,5},{8,10},{9,11},{10,... | collective-permute-start | bytes 1572872 | tf_op jit(solution)/shard_map/ppermute | solution.py:37
  0.7 0.4 copy-done.4
  1.1 1.3 %collective-permute-start.2 = (bf16[2,2,64,256]{3,2,1,0:T(8,128)(2,1)S(1)}, bf16[2,2,64,256]{3,2,1,0:T(8,128)(2,1)S(1)}, u32[]{:S(2)}, u32[]{:S(2)}) collective-permute-start(bf16[2,2,64,256]{3,2,1,0:T(8,128)(2,1)S(1)} %get-tuple-element.25), channel_id=1, source_target_pairs={{0,1},{1,0},{2,3},{3,2},{4,5},{5,4},{6,7},{7,6},{8,9},{9,8},{10,11... | collective-permute-start | bytes 393224 | tf_op jit(solution)/shard_map/ppermute | solution.py:37
  2.4 2.1 %collective-permute-start = (bf16[8,64,256]{2,1,0:T(8,128)(2,1)S(1)}, bf16[8,64,256]{2,1,0:T(8,128)(2,1)S(1)}, u32[]{:S(2)}, u32[]{:S(2)}) collective-permute-start(bf16[8,64,256]{2,1,0:T(8,128)(2,1)S(1)} %get-tuple-element.23), channel_id=1, source_target_pairs={{0,1},{1,0},{2,4},{3,5},{4,2},{5,3},{6,8},{7,9},{8,6},{9,7},{10,12... | collective-permute-start | bytes 786440 | tf_op jit(solution)/shard_map/ppermute | solution.py:37
  4.5 0.6 %collective-permute-start.1 = (bf16[8,64,256]{2,1,0:T(8,128)(2,1)S(1)}, bf16[8,64,256]{2,1,0:T(8,128)(2,1)S(1)}, u32[]{:S(2)}, u32[]{:S(2)}) collective-permute-start(bf16[8,64,256]{2,1,0:T(8,128)(2,1)S(1)} %get-tuple-element.24), channel_id=1, source_target_pairs={{0,1},{1,0},{2,4},{3,5},{4,2},{5,3},{6,8},{7,9},{8,6},{9,7},{10,12... | collective-permute-start | bytes 786440 | tf_op jit(solution)/shard_map/ppermute | solution.py:37
  5.0 0.5 %collective-permute-done.2.refs_1_ = bf16[2,2,64,256]{3,2,1,0:T(8,128)(2,1)S(1)} collective-permute-done((bf16[2,2,64,256]{3,2,1,0:T(8,128)(2,1)S(1)}, bf16[2,2,64,256]{3,2,1,0:T(8,128)(2,1)S(1)}, u32[]{:S(2)}, u32[]{:S(2)}) %collective-permute-start.2) | collective-permute-done | bytes 131104 | tf_op jit(solution)/shard_map/ppermute | solution.py:37
  5.5 1.5 %collective-permute-start.5 = (bf16[2,2,64,256]{3,2,1,0:T(8,128)(2,1)S(1)}, bf16[2,2,64,256]{3,2,1,0:T(8,128)(2,1)S(1)}, u32[]{:S(2)}, u32[]{:S(2)}) collective-permute-start(bf16[2,2,64,256]{3,2,1,0:T(8,128)(2,1)S(1)} %collective-permute-done.2.refs_1_), channel_id=1, source_target_pairs={{0,2},{1,3},{2,0},{3,1},{4,6},{5,7},{6,4},{7,5},{8,10},{9,11},{10,... | collective-permute-start | bytes 393224 | tf_op jit(solution)/shard_map/ppermute | solution.py:37
  7.1 1.1 %collective-permute-start.3 = (bf16[2,2,64,256]{3,2,1,0:T(8,128)(2,1)S(1)}, bf16[2,2,64,256]{3,2,1,0:T(8,128)(2,1)S(1)}, u32[]{:S(2)}, u32[]{:S(2)}) collective-permute-start(bf16[2,2,64,256]{3,2,1,0:T(8,128)(2,1)S(1)} %collective-permute-done.2.refs_1_), channel_id=1, source_target_pairs={{0,1},{1,0},{2,4},{3,5},{4,2},{5,3},{6,8},{7,9},{8,6},{9,7},{10,12... | collective-permute-start | bytes 393224 | tf_op jit(solution)/shard_map/ppermute | solution.py:37
  8.2 0.0 collective-permute-done.4.near.refs_2_
  8.2 5.0 %shard_map.57 = (bf16[7,64,256]{2,1,0:T(8,128)(2,1)S(1)}, bf16[7,64,256]{2,1,0:T(8,128)(2,1)S(1)}, f32[7,64,256]{2,1,0:T(8,128)S(1)}, f32[7,64,256]{2,1,0:T(8,128)S(1)}) custom-call(bf16[2,8,64,256]{3,2,1,0:T(8,128)(2,1)S(1)} %copy-done.4, bf16[2,8,64,256]{3,2,1,0:T(8,128)(2,1)S(1)} %collective-permute-done.4.near.refs_2_, ...), custom_call_target="tpu_custom_call" | custom-call | flops 4756340736 | bytes 1048576 | tf_op jit(solution)/shard_map/pallas_call | solution.py:66
  13.2 0.0 collective-permute-done.5.refs_3_
  13.3 3.4 %shard_map.59 = (f32[8,64,256]{2,1,0:T(8,128)S(1)}, f32[8,64,256]{2,1,0:T(8,128)S(1)}, f32[2,64,256]{2,1,0:T(8,128)S(1)}, f32[2,64,256]{2,1,0:T(8,128)S(1)}) custom-call(bf16[2,8,64,256]{3,2,1,0:T(8,128)(2,1)S(1)} %copy-done.4, bf16[2,2,64,256]{3,2,1,0:T(8,128)(2,1)S(1)} %collective-permute-done.2.refs_1_, ...), custom_call_target="tpu_custom_call" | custom-call | flops 3170893824 | bytes 1048576 | tf_op jit(solution)/shard_map/pallas_call | solution.py:66
  16.7 0.0 collective-permute-done.plane_one.refs_0_
  16.7 0.0 collective-permute-done.1.plane_zero.refs_1_
  16.7 1.9 %shard_map.58 = (bf16[7,64,256]{2,1,0:T(8,128)(2,1)S(1)}, bf16[7,64,256]{2,1,0:T(8,128)(2,1)S(1)}) custom-call(bf16[8,64,256]{2,1,0:T(8,128)(2,1)S(1)} %collective-permute-done.plane_one.refs_0_, bf16[8,64,256]{2,1,0:T(8,128)(2,1)S(1)} %collective-permute-done.1.plane_zero.refs_1_, f32[7,64,256]{2,1,0:T(8,128)S(1)} %get-tuple-element.26.part_one, ...), custom_call_target="tpu_custom_call" | custom-call | flops 1585446912 | bytes 1048576 | tf_op jit(solution)/shard_map/pallas_call | solution.py:66
  18.6 0.0 copy-start
  18.6 2.8 %shard_map.60 = (bf16[8,64,256]{2,1,0:T(8,128)(2,1)S(1)}, bf16[8,64,256]{2,1,0:T(8,128)(2,1)S(1)}, bf16[4,32,256]{2,1,0:T(8,128)(2,1)S(1)}) custom-call(bf16[8,64,256]{2,1,0:T(8,128)(2,1)S(1)} %collective-permute-done.plane_one.refs_0_, bf16[8,64,256]{2,1,0:T(8,128)(2,1)S(1)} %collective-permute-done.1.plane_zero.refs_1_, ...), custom_call_target="tpu_custom_call" | custom-call | flops 2264924160 | bytes 1048576 | tf_op jit(solution)/shard_map/pallas_call | solution.py:66
  21.4 0.0 copy-start.3
  21.4 1.3 %collective-permute-start.8 = (bf16[4,32,256]{2,1,0:T(8,128)(2,1)S(1)}, bf16[4,32,256]{2,1,0:T(8,128)(2,1)S(1)}, u32[]{:S(2)}, u32[]{:S(2)}) collective-permute-start(bf16[4,32,256]{2,1,0:T(8,128)(2,1)S(1)} %get-tuple-element.38.refs_0_), channel_id=1, source_target_pairs={{0,1},{1,0},{2,3},{3,2},{4,5},{5,4},{6,7},{7,6},{8,9},{9,8},{10,11... | collective-permute-start | bytes 196616 | tf_op jit(solution)/shard_map/ppermute | solution.py:37
  22.7 1.6 %collective-permute-start.9 = (bf16[4,32,256]{2,1,0:T(8,128)(2,1)S(1)}, bf16[4,32,256]{2,1,0:T(8,128)(2,1)S(1)}, u32[]{:S(2)}, u32[]{:S(2)}) collective-permute-start(bf16[4,32,256]{2,1,0:T(8,128)(2,1)S(1)} %get-tuple-element.38.refs_0_), channel_id=1, source_target_pairs={{0,2},{1,3},{2,0},{3,1},{4,6},{5,7},{6,4},{7,5},{8,10},{9,11},{10,... | collective-permute-start | bytes 196616 | tf_op jit(solution)/shard_map/ppermute | solution.py:37
  24.2 0.3 collective-permute-done.8.refs_1_
  24.6 3.4 %collective-permute-start.10 = (bf16[4,32,256]{2,1,0:T(8,128)(2,1)S(1)}, bf16[4,32,256]{2,1,0:T(8,128)(2,1)S(1)}, u32[]{:S(2)}, u32[]{:S(2)}) collective-permute-start(bf16[4,32,256]{2,1,0:T(8,128)(2,1)S(1)} %collective-permute-done.8.refs_1_), channel_id=1, source_target_pairs={{0,2},{1,3},{2,0},{3,1},{4,6},{5,7},{6,4},{7,5},{8,10},{9,11},{10,... | collective-permute-start | bytes 196616 | tf_op jit(solution)/shard_map/ppermute | solution.py:37
  28.0 0.7 %collective-permute-start.7 = (bf16[4,32,256]{2,1,0:T(8,128)(2,1)S(1)}, bf16[4,32,256]{2,1,0:T(8,128)(2,1)S(1)}, u32[]{:S(2)}, u32[]{:S(2)}) collective-permute-start(bf16[4,32,256]{2,1,0:T(8,128)(2,1)S(1)} %get-tuple-element.38.refs_0_), channel_id=1, source_target_pairs={{0,1},{1,0},{2,5},{3,4},{4,3},{5,2},{6,9},{7,8},{8,7},{9,6},{10,13... | collective-permute-start | bytes 196616 | tf_op jit(solution)/shard_map/ppermute | solution.py:37
  28.7 1.9 %collective-permute-start.6 = (bf16[4,32,256]{2,1,0:T(8,128)(2,1)S(1)}, bf16[4,32,256]{2,1,0:T(8,128)(2,1)S(1)}, u32[]{:S(2)}, u32[]{:S(2)}) collective-permute-start(bf16[4,32,256]{2,1,0:T(8,128)(2,1)S(1)} %get-tuple-element.38.refs_0_), channel_id=1, source_target_pairs={{0,1},{1,0},{2,4},{3,5},{4,2},{5,3},{6,8},{7,9},{8,6},{9,7},{10,12... | collective-permute-start | bytes 196616 | tf_op jit(solution)/shard_map/ppermute | solution.py:37
  30.6 0.0 collective-permute-done.9.refs_2_
  30.6 0.0 collective-permute-done.10.refs_3_
  30.6 0.8 %shard_map.61.refs_2_ = f32[8,32,256]{2,1,0:T(8,128)S(1)} custom-call(bf16[4,32,256]{2,1,0:T(8,128)(2,1)S(1)} %get-tuple-element.38.refs_0_, bf16[4,32,256]{2,1,0:T(8,128)(2,1)S(1)} %collective-permute-done.8.refs_1_, bf16[4,32,256]{2,1,0:T(8,128)(2,1)S(1)} %collective-permute-done.9.refs_2_, bf16[4,32,256]{2,1,0:T(8,128)(2,1)S(1)} %collective-permute-done.10.refs_3_, ...), custom_call_target="tpu_custom_call" | custom-call | flops 603979776 | bytes 1048576 | tf_op jit(solution)/shard_map/pallas_call | solution.py:66
  31.4 2.6 %collective-permute-done.7.refs_1_ = bf16[4,32,256]{2,1,0:T(8,128)(2,1)S(1)} collective-permute-done((bf16[4,32,256]{2,1,0:T(8,128)(2,1)S(1)}, bf16[4,32,256]{2,1,0:T(8,128)(2,1)S(1)}, u32[]{:S(2)}, u32[]{:S(2)}) %collective-permute-start.7) | collective-permute-done | bytes 65568 | tf_op jit(solution)/shard_map/ppermute | solution.py:37
  34.0 0.7 %shard_map.62 = (f32[4,32,256]{2,1,0:T(8,128)S(1)}, bf16[4,32,256]{2,1,0:T(8,128)(2,1)S(1)}) custom-call(bf16[4,32,256]{2,1,0:T(8,128)(2,1)S(1)} %collective-permute-done.6.refs_0_, bf16[4,32,256]{2,1,0:T(8,128)(2,1)S(1)} %collective-permute-done.7.refs_1_, f32[8,32,256]{2,1,0:T(8,128)S(1)} %shard_map.61.refs_2_, bf16[3,3,3,256,256]{4,3,2,1,0:T(8,128)(2,1)S(1)} %copy-done, ...), custom_call_target="tpu_custom_call" | custom-call | flops 301989888 | bytes 1048576 | tf_op jit(solution)/shard_map/pallas_call | solution.py:66
  34.7 0.5 %collective-permute-start.11 = (bf16[4,32,256]{2,1,0:T(8,128)(2,1)S(1)}, bf16[4,32,256]{2,1,0:T(8,128)(2,1)S(1)}, u32[]{:S(2)}, u32[]{:S(2)}) collective-permute-start(bf16[4,32,256]{2,1,0:T(8,128)(2,1)S(1)} %get-tuple-element.40), channel_id=1, source_target_pairs={{0,1},{1,0},{2,3},{3,2},{4,5},{5,4},{6,7},{7,6},{8,9},{9,8},{10,11... | collective-permute-start | bytes 196616 | tf_op jit(solution)/shard_map/ppermute | solution.py:37
  35.2 2.7 %collective-permute-done.11.refs_3_ = bf16[4,32,256]{2,1,0:T(8,128)(2,1)S(1)} collective-permute-done((bf16[4,32,256]{2,1,0:T(8,128)(2,1)S(1)}, bf16[4,32,256]{2,1,0:T(8,128)(2,1)S(1)}, u32[]{:S(2)}, u32[]{:S(2)}) %collective-permute-start.11) | collective-permute-done | bytes 65568 | tf_op jit(solution)/shard_map/ppermute | solution.py:37
  37.9 0.9 %shard_map.63 = bf16[2,8,64,256]{3,2,1,0:T(8,128)(2,1)} custom-call(bf16[8,64,256]{2,1,0:T(8,128)(2,1)S(1)} %get-tuple-element.36.refs_0_, bf16[8,64,256]{2,1,0:T(8,128)(2,1)S(1)} %get-tuple-element.37.refs_1_, f32[4,32,256]{2,1,0:T(8,128)S(1)} %get-tuple-element.39.refs_2_, bf16[4,32,256]{2,1,0:T(8,128)(2,1)S(1)} %collective-permute-done.11.refs_3_), custom_call_target="tpu_custom_call" | custom-call | flops 262144 | bytes 1048576 | tf_op jit(solution)/shard_map/pallas_call | solution.py:66
  (11 shorter events, 0.1 us)
Async XLA Ops:
  0.0 1.0 %copy-start.4 = (bf16[2,8,64,256]{3,2,1,0:T(8,128)(2,1)S(1)}, bf16[2,8,64,256]{3,2,1,0:T(8,128)(2,1)}, u32[]{:S(2)}) copy-start(bf16[2,8,64,256]{3,2,1,0:T(8,128)(2,1)} %refs_0_.1) | copy-start | bytes 1572868
  0.0 8.2 %collective-permute-start.4 = (bf16[2,8,64,256]{3,2,1,0:T(8,128)(2,1)}, bf16[2,8,64,256]{3,2,1,0:T(8,128)(2,1)S(1)}, u32[]{:S(2)}, u32[]{:S(2)}) collective-permute-start(bf16[2,8,64,256]{3,2,1,0:T(8,128)(2,1)} %refs_0_.1), channel_id=1, source_target_pairs={{0,2},{1,3},{2,0},{3,1},{4,6},{5,7},{6,4},{7,5},{8,10},{9,11},{10,... | collective-permute-start | bytes 1572872 | tf_op jit(solution)/shard_map/ppermute | solution.py:37
  1.0 7.2 %copy-start.1 = (bf16[3,3,3,256,256]{4,3,2,1,0:T(8,128)(2,1)S(1)}, bf16[3,3,3,256,256]{4,3,2,1,0:T(8,128)(2,1)}, u32[]{:S(2)}) copy-start(bf16[3,3,3,256,256]{4,3,2,1,0:T(8,128)(2,1)} %refs_7_.3) | copy-start | bytes 10616836
  1.1 4.4 %collective-permute-start.2 = (bf16[2,2,64,256]{3,2,1,0:T(8,128)(2,1)S(1)}, bf16[2,2,64,256]{3,2,1,0:T(8,128)(2,1)S(1)}, u32[]{:S(2)}, u32[]{:S(2)}) collective-permute-start(bf16[2,2,64,256]{3,2,1,0:T(8,128)(2,1)S(1)} %get-tuple-element.25), channel_id=1, source_target_pairs={{0,1},{1,0},{2,3},{3,2},{4,5},{5,4},{6,7},{7,6},{8,9},{9,8},{10,11... | collective-permute-start | bytes 393224 | tf_op jit(solution)/shard_map/ppermute | solution.py:37
  2.4 14.3 %collective-permute-start = (bf16[8,64,256]{2,1,0:T(8,128)(2,1)S(1)}, bf16[8,64,256]{2,1,0:T(8,128)(2,1)S(1)}, u32[]{:S(2)}, u32[]{:S(2)}) collective-permute-start(bf16[8,64,256]{2,1,0:T(8,128)(2,1)S(1)} %get-tuple-element.23), channel_id=1, source_target_pairs={{0,1},{1,0},{2,4},{3,5},{4,2},{5,3},{6,8},{7,9},{8,6},{9,7},{10,12... | collective-permute-start | bytes 786440 | tf_op jit(solution)/shard_map/ppermute | solution.py:37
  4.4 8.8 %copy-start.2 = (bf16[3,3,3,256,256]{4,3,2,1,0:T(8,128)(2,1)S(1)}, bf16[3,3,3,256,256]{4,3,2,1,0:T(8,128)(2,1)}, u32[]{:S(2)}) copy-start(bf16[3,3,3,256,256]{4,3,2,1,0:T(8,128)(2,1)} %refs_8_.1) | copy-start | bytes 10616836
  4.5 12.2 %collective-permute-start.1 = (bf16[8,64,256]{2,1,0:T(8,128)(2,1)S(1)}, bf16[8,64,256]{2,1,0:T(8,128)(2,1)S(1)}, u32[]{:S(2)}, u32[]{:S(2)}) collective-permute-start(bf16[8,64,256]{2,1,0:T(8,128)(2,1)S(1)} %get-tuple-element.24), channel_id=1, source_target_pairs={{0,1},{1,0},{2,4},{3,5},{4,2},{5,3},{6,8},{7,9},{8,6},{9,7},{10,12... | collective-permute-start | bytes 786440 | tf_op jit(solution)/shard_map/ppermute | solution.py:37
  5.5 7.7 %collective-permute-start.5 = (bf16[2,2,64,256]{3,2,1,0:T(8,128)(2,1)S(1)}, bf16[2,2,64,256]{3,2,1,0:T(8,128)(2,1)S(1)}, u32[]{:S(2)}, u32[]{:S(2)}) collective-permute-start(bf16[2,2,64,256]{3,2,1,0:T(8,128)(2,1)S(1)} %collective-permute-done.2.refs_1_), channel_id=1, source_target_pairs={{0,2},{1,3},{2,0},{3,1},{4,6},{5,7},{6,4},{7,5},{8,10},{9,11},{10,... | collective-permute-start | bytes 393224 | tf_op jit(solution)/shard_map/ppermute | solution.py:37
  7.1 11.5 %collective-permute-start.3 = (bf16[2,2,64,256]{3,2,1,0:T(8,128)(2,1)S(1)}, bf16[2,2,64,256]{3,2,1,0:T(8,128)(2,1)S(1)}, u32[]{:S(2)}, u32[]{:S(2)}) collective-permute-start(bf16[2,2,64,256]{3,2,1,0:T(8,128)(2,1)S(1)} %collective-permute-done.2.refs_1_), channel_id=1, source_target_pairs={{0,1},{1,0},{2,4},{3,5},{4,2},{5,3},{6,8},{7,9},{8,6},{9,7},{10,12... | collective-permute-start | bytes 393224 | tf_op jit(solution)/shard_map/ppermute | solution.py:37
  18.6 12.0 %copy-start = (bf16[3,3,3,256,256]{4,3,2,1,0:T(8,128)(2,1)S(1)}, bf16[3,3,3,256,256]{4,3,2,1,0:T(8,128)(2,1)}, u32[]{:S(2)}) copy-start(bf16[3,3,3,256,256]{4,3,2,1,0:T(8,128)(2,1)} %refs_3_.1) | copy-start | bytes 10616836
  21.4 12.6 %copy-start.3 = (bf16[256,256]{1,0:T(8,128)(2,1)S(1)}, bf16[256,256]{1,0:T(8,128)(2,1)}, u32[]{:S(2)}) copy-start(bf16[256,256]{1,0:T(8,128)(2,1)} %refs_4_.3) | copy-start | bytes 393220
  21.4 3.2 %collective-permute-start.8 = (bf16[4,32,256]{2,1,0:T(8,128)(2,1)S(1)}, bf16[4,32,256]{2,1,0:T(8,128)(2,1)S(1)}, u32[]{:S(2)}, u32[]{:S(2)}) collective-permute-start(bf16[4,32,256]{2,1,0:T(8,128)(2,1)S(1)} %get-tuple-element.38.refs_0_), channel_id=1, source_target_pairs={{0,1},{1,0},{2,3},{3,2},{4,5},{5,4},{6,7},{7,6},{8,9},{9,8},{10,11... | collective-permute-start | bytes 196616 | tf_op jit(solution)/shard_map/ppermute | solution.py:37
  22.7 7.9 %collective-permute-start.9 = (bf16[4,32,256]{2,1,0:T(8,128)(2,1)S(1)}, bf16[4,32,256]{2,1,0:T(8,128)(2,1)S(1)}, u32[]{:S(2)}, u32[]{:S(2)}) collective-permute-start(bf16[4,32,256]{2,1,0:T(8,128)(2,1)S(1)} %get-tuple-element.38.refs_0_), channel_id=1, source_target_pairs={{0,2},{1,3},{2,0},{3,1},{4,6},{5,7},{6,4},{7,5},{8,10},{9,11},{10,... | collective-permute-start | bytes 196616 | tf_op jit(solution)/shard_map/ppermute | solution.py:37
  24.6 6.0 %collective-permute-start.10 = (bf16[4,32,256]{2,1,0:T(8,128)(2,1)S(1)}, bf16[4,32,256]{2,1,0:T(8,128)(2,1)S(1)}, u32[]{:S(2)}, u32[]{:S(2)}) collective-permute-start(bf16[4,32,256]{2,1,0:T(8,128)(2,1)S(1)} %collective-permute-done.8.refs_1_), channel_id=1, source_target_pairs={{0,2},{1,3},{2,0},{3,1},{4,6},{5,7},{6,4},{7,5},{8,10},{9,11},{10,... | collective-permute-start | bytes 196616 | tf_op jit(solution)/shard_map/ppermute | solution.py:37
  28.0 6.0 %collective-permute-start.7 = (bf16[4,32,256]{2,1,0:T(8,128)(2,1)S(1)}, bf16[4,32,256]{2,1,0:T(8,128)(2,1)S(1)}, u32[]{:S(2)}, u32[]{:S(2)}) collective-permute-start(bf16[4,32,256]{2,1,0:T(8,128)(2,1)S(1)} %get-tuple-element.38.refs_0_), channel_id=1, source_target_pairs={{0,1},{1,0},{2,5},{3,4},{4,3},{5,2},{6,9},{7,8},{8,7},{9,6},{10,13... | collective-permute-start | bytes 196616 | tf_op jit(solution)/shard_map/ppermute | solution.py:37
  28.7 5.3 %collective-permute-start.6 = (bf16[4,32,256]{2,1,0:T(8,128)(2,1)S(1)}, bf16[4,32,256]{2,1,0:T(8,128)(2,1)S(1)}, u32[]{:S(2)}, u32[]{:S(2)}) collective-permute-start(bf16[4,32,256]{2,1,0:T(8,128)(2,1)S(1)} %get-tuple-element.38.refs_0_), channel_id=1, source_target_pairs={{0,1},{1,0},{2,4},{3,5},{4,2},{5,3},{6,8},{7,9},{8,6},{9,7},{10,12... | collective-permute-start | bytes 196616 | tf_op jit(solution)/shard_map/ppermute | solution.py:37
  34.7 3.2 %collective-permute-start.11 = (bf16[4,32,256]{2,1,0:T(8,128)(2,1)S(1)}, bf16[4,32,256]{2,1,0:T(8,128)(2,1)S(1)}, u32[]{:S(2)}, u32[]{:S(2)}) collective-permute-start(bf16[4,32,256]{2,1,0:T(8,128)(2,1)S(1)} %get-tuple-element.40), channel_id=1, source_target_pairs={{0,1},{1,0},{2,3},{3,2},{4,5},{5,4},{6,7},{7,6},{8,9},{9,8},{10,11... | collective-permute-start | bytes 196616 | tf_op jit(solution)/shard_map/ppermute | solution.py:37

commit v3 on v2

--- a/solution.py
+++ b/solution.py
@@ -195,19 +195,28 @@
         out_three[spot] = conv_lines([(layer, 0, tap(1, odd)), (layer, 1, tap(2, odd))], row, lines, weight_two)
 
 
-def kernel_b0(plane_one, plane_zero, part_one, part_two, weight_one, done_one, done_two, field, *, chans):
-    odd = lax.rem(lax.axis_index("brick"), 2)
-    valid = has_far()
-    fill_inner(field, ((plane_zero, None), (plane_one, None)), valid)
+def kernel_m(plane_one, part_one, part_two, weight_one, more_one, done_two, field, *, chans):
+    odd = lax.rem(lax.axis_index("brick"), 2)
+    fill_inner(field, ((plane_one, None),), has_far())
     first, rows = inner_rows(chans, plane_one.shape[0])
     lines = tile_of(rows)
     for row in range(0, rows, lines):
         spot, base = pl.ds(row, lines), first + row
-        value = conv_lines([(field, 0, tap(0, odd)), (field, 1, tap(1, odd))], base, lines, weight_one)
-        value = jnp.maximum(value + part_one[spot], 0.0)
-        done_one[spot] = jnp.where(valid, value, 0.0).astype(BF16)
-        value = conv_lines([(field, 1, tap(0, odd))], base, lines, weight_one)
+        value = conv_lines([(field, 0, tap(0, odd))], base, lines, weight_one)
         done_two[spot] = jnp.maximum(value + part_two[spot], 0.0).astype(BF16)
+        more_one[spot] = part_one[spot] + conv_lines([(field, 0, tap(1, odd))], base, lines, weight_one)
+
+
+def kernel_b0(plane_zero, part_one, weight_one, done_one, field, *, chans):
+    odd = lax.rem(lax.axis_index("brick"), 2)
+    valid = has_far()
+    fill_inner(field, ((plane_zero, None),), valid)
+    first, rows = inner_rows(chans, plane_zero.shape[0])
+    lines = tile_of(rows)
+    for row in range(0, rows, lines):
+        spot = pl.ds(row, lines)
+        value = conv_lines([(field, 0, tap(0, odd))], first + row, lines, weight_one)
+        done_one[spot] = jnp.where(valid, jnp.maximum(value + part_one[spot], 0.0), 0.0).astype(BF16)
 
 
 def kernel_b1(*refs, chans, sides):
@@ -353,6 +362,14 @@
         9 * inner * line_flops,
         12,
     )
+    part_one, done_two = call(
+        functools.partial(kernel_m, chans=chans),
+        [far_one, part_one, part_two, first_weight],
+        [((inner, depth, channels), F32), ((inner, depth, channels), BF16)],
+        [pltpu.VMEM((1, size_y + 2, depth, channels), BF16)],
+        2 * inner * line_flops,
+        12,
+    )
     out_two, out_three, *border = call(
         functools.partial(kernel_a1, **static),
         [volume, *own_halos, near, *near_halos, done_three, done_four, first_weight, second_weight],
@@ -361,14 +378,14 @@
         (18 * sides + 3 * size_y) * line_flops,
         12,
     )
-    done_one, done_two = call(
+    done_one = call(
         functools.partial(kernel_b0, chans=chans),
-        [far_one, far_zero, part_one, part_two, first_weight],
-        [((inner, depth, channels), BF16)] * 2,
-        [pltpu.VMEM((2, size_y + 2, depth, channels), BF16)],
-        3 * inner * line_flops,
-        12,
-    )
+        [far_zero, part_one, first_weight],
+        [((inner, depth, channels), BF16)],
+        [pltpu.VMEM((1, size_y + 2, depth, channels), BF16)],
+        inner * line_flops,
+        12,
+    )[0]
     skipped_two, skipped_three, pooled = call(
         functools.partial(kernel_b1, **static),
         [far_one, far_zero, *far_halos, done_one, done_two, out_two, out_three, first_weight, second_weight, *border],

time: 39.6 us -> 39.2 us (0.990)
  the two profiles are of different devices: /device:TPU:21 before, /device:TPU:26 now
where the time goes in v3:
time: 39.2 us; the launch traced here: 39.1 us
  Pallas kernels  15.6 us (40%)
  waiting for transfers between devices  12.8 us (33%)
  starting transfers between devices  9.45 us (24%)
  local copies, waits for them, and re-layouts  1.05 us (3%)
    pallas_call x10, Pallas kernels, call(): pl.pallas_call(kernel, out_shape=out_shape, in_specs=[VMEM_SPEC] * len(in...  15.6 us
    ppermute x12, waiting for transfers between devices, exchange(): return lax.ppermute(value, AXES, pairs)  12.8 us
    ppermute x12, starting transfers between devices, exchange(): return lax.ppermute(value, AXES, pairs)  9.45 us
    unnamed x10, local copies, waits for them, and re-layouts  1.05 us
  transfers between devices with their start and end apart: 12, of which 5 were waited for; matrix products, arithmetic and copies ran while one was open for 0% of the time, Pallas kernels for 29%

profile of v3, /device:TPU:26, one launch (start us, length us, event | category | flops | bytes accessed | tf_op | source)
XLA Modules:
  0.0 39.1 jit_solution(7266018052538763760)
XLA Ops:
  0.0 0.0 collective-permute-start.4
  0.0 1.0 %copy-done.4 = bf16[2,8,64,256]{3,2,1,0:T(8,128)(2,1)S(1)} copy-done((bf16[2,8,64,256]{3,2,1,0:T(8,128)(2,1)S(1)}, bf16[2,8,64,256]{3,2,1,0:T(8,128)(2,1)}, u32[]{:S(2)}) %copy-start.4) | copy-done | bytes 524312
  1.1 0.6 %collective-permute-start.2 = (bf16[2,2,64,256]{3,2,1,0:T(8,128)(2,1)S(1)}, bf16[2,2,64,256]{3,2,1,0:T(8,128)(2,1)S(1)}, u32[]{:S(2)}, u32[]{:S(2)}) collective-permute-start(bf16[2,2,64,256]{3,2,1,0:T(8,128)(2,1)S(1)} %get-tuple-element.25), channel_id=1, source_target_pairs={{0,1},{1,0},{2,3},{3,2},{4,5},{5,4},{6,7},{7,6},{8,9},{9,8},{10,11... | collective-permute-start | bytes 393224 | tf_op jit(solution)/shard_map/ppermute | solution.py:37
  1.7 0.6 %collective-permute-start = (bf16[8,64,256]{2,1,0:T(8,128)(2,1)S(1)}, bf16[8,64,256]{2,1,0:T(8,128)(2,1)S(1)}, u32[]{:S(2)}, u32[]{:S(2)}) collective-permute-start(bf16[8,64,256]{2,1,0:T(8,128)(2,1)S(1)} %get-tuple-element.23), channel_id=1, source_target_pairs={{0,1},{1,0},{2,4},{3,5},{4,2},{5,3},{6,8},{7,9},{8,6},{9,7},{10,12... | collective-permute-start | bytes 786440 | tf_op jit(solution)/shard_map/ppermute | solution.py:37
  2.3 2.1 %collective-permute-start.1 = (bf16[8,64,256]{2,1,0:T(8,128)(2,1)S(1)}, bf16[8,64,256]{2,1,0:T(8,128)(2,1)S(1)}, u32[]{:S(2)}, u32[]{:S(2)}) collective-permute-start(bf16[8,64,256]{2,1,0:T(8,128)(2,1)S(1)} %get-tuple-element.24), channel_id=1, source_target_pairs={{0,1},{1,0},{2,4},{3,5},{4,2},{5,3},{6,8},{7,9},{8,6},{9,7},{10,12... | collective-permute-start | bytes 786440 | tf_op jit(solution)/shard_map/ppermute | solution.py:37
  4.3 2.1 %collective-permute-done.2.refs_1_ = bf16[2,2,64,256]{3,2,1,0:T(8,128)(2,1)S(1)} collective-permute-done((bf16[2,2,64,256]{3,2,1,0:T(8,128)(2,1)S(1)}, bf16[2,2,64,256]{3,2,1,0:T(8,128)(2,1)S(1)}, u32[]{:S(2)}, u32[]{:S(2)}) %collective-permute-start.2) | collective-permute-done | bytes 131104 | tf_op jit(solution)/shard_map/ppermute | solution.py:37
  6.4 0.0 collective-permute-start.5
  6.4 1.5 %collective-permute-start.3 = (bf16[2,2,64,256]{3,2,1,0:T(8,128)(2,1)S(1)}, bf16[2,2,64,256]{3,2,1,0:T(8,128)(2,1)S(1)}, u32[]{:S(2)}, u32[]{:S(2)}) collective-permute-start(bf16[2,2,64,256]{3,2,1,0:T(8,128)(2,1)S(1)} %collective-permute-done.2.refs_1_), channel_id=1, source_target_pairs={{0,1},{1,0},{2,4},{3,5},{4,2},{5,3},{6,8},{7,9},{8,6},{9,7},{10,12... | collective-permute-start | bytes 393224 | tf_op jit(solution)/shard_map/ppermute | solution.py:37
  7.9 0.0 collective-permute-done.4.near.refs_2_
  7.9 5.0 %shard_map.57 = (bf16[7,64,256]{2,1,0:T(8,128)(2,1)S(1)}, bf16[7,64,256]{2,1,0:T(8,128)(2,1)S(1)}, f32[7,64,256]{2,1,0:T(8,128)S(1)}, f32[7,64,256]{2,1,0:T(8,128)S(1)}) custom-call(bf16[2,8,64,256]{3,2,1,0:T(8,128)(2,1)S(1)} %copy-done.4, bf16[2,8,64,256]{3,2,1,0:T(8,128)(2,1)S(1)} %collective-permute-done.4.near.refs_2_, ...), custom_call_target="tpu_custom_call" | custom-call | flops 4756340736 | bytes 1048576 | tf_op jit(solution)/shard_map/pallas_call | solution.py:66
  13.0 0.0 collective-permute-done.5.refs_3_
  13.0 3.4 %shard_map.60 = (f32[8,64,256]{2,1,0:T(8,128)S(1)}, f32[8,64,256]{2,1,0:T(8,128)S(1)}, f32[2,64,256]{2,1,0:T(8,128)S(1)}, f32[2,64,256]{2,1,0:T(8,128)S(1)}) custom-call(bf16[2,8,64,256]{3,2,1,0:T(8,128)(2,1)S(1)} %copy-done.4, bf16[2,2,64,256]{3,2,1,0:T(8,128)(2,1)S(1)} %collective-permute-done.2.refs_1_, ...), custom_call_target="tpu_custom_call" | custom-call | flops 3170893824 | bytes 1048576 | tf_op jit(solution)/shard_map/pallas_call | solution.py:66
  16.4 1.3 %shard_map.58 = (f32[7,64,256]{2,1,0:T(8,128)S(1)}, bf16[7,64,256]{2,1,0:T(8,128)(2,1)S(1)}) custom-call(bf16[8,64,256]{2,1,0:T(8,128)(2,1)S(1)} %collective-permute-done.plane_one.refs_0_, f32[7,64,256]{2,1,0:T(8,128)S(1)} %get-tuple-element.26.part_one, f32[7,64,256]{2,1,0:T(8,128)S(1)} %get-tuple-element.27.part_two, bf16[3,3,3,256,256]{4,3,2,1,0:T(8,128)(2,1)S(1)} %copy-done), custom_call_target="tpu_custom_call" | custom-call | flops 1056964608 | bytes 1048576 | tf_op jit(solution)/shard_map/pallas_call | solution.py:66
  17.7 0.7 %shard_map.59.refs_3_ = bf16[7,64,256]{2,1,0:T(8,128)(2,1)S(1)} custom-call(bf16[8,64,256]{2,1,0:T(8,128)(2,1)S(1)} %collective-permute-done.1.plane_zero.refs_1_, f32[7,64,256]{2,1,0:T(8,128)S(1)} %get-tuple-element.28.part_one, bf16[3,3,3,256,256]{4,3,2,1,0:T(8,128)(2,1)S(1)} %copy-done), custom_call_target="tpu_custom_call" | custom-call | flops 528482304 | bytes 1048576 | tf_op jit(solution)/shard_map/pallas_call | solution.py:66
  18.5 0.0 copy-start.1
  18.5 2.8 %shard_map.61 = (bf16[8,64,256]{2,1,0:T(8,128)(2,1)S(1)}, bf16[8,64,256]{2,1,0:T(8,128)(2,1)S(1)}, bf16[4,32,256]{2,1,0:T(8,128)(2,1)S(1)}) custom-call(bf16[8,64,256]{2,1,0:T(8,128)(2,1)S(1)} %collective-permute-done.plane_one.refs_0_, bf16[8,64,256]{2,1,0:T(8,128)(2,1)S(1)} %collective-permute-done.1.plane_zero.refs_1_, ...), custom_call_target="tpu_custom_call" | custom-call | flops 2264924160 | bytes 1048576 | tf_op jit(solution)/shard_map/pallas_call | solution.py:66
  21.2 0.0 copy-start.3
  21.2 0.6 %collective-permute-start.8 = (bf16[4,32,256]{2,1,0:T(8,128)(2,1)S(1)}, bf16[4,32,256]{2,1,0:T(8,128)(2,1)S(1)}, u32[]{:S(2)}, u32[]{:S(2)}) collective-permute-start(bf16[4,32,256]{2,1,0:T(8,128)(2,1)S(1)} %get-tuple-element.38.refs_0_), channel_id=1, source_target_pairs={{0,1},{1,0},{2,3},{3,2},{4,5},{5,4},{6,7},{7,6},{8,9},{9,8},{10,11... | collective-permute-start | bytes 196616 | tf_op jit(solution)/shard_map/ppermute | solution.py:37
  21.8 1.0 %collective-permute-start.9 = (bf16[4,32,256]{2,1,0:T(8,128)(2,1)S(1)}, bf16[4,32,256]{2,1,0:T(8,128)(2,1)S(1)}, u32[]{:S(2)}, u32[]{:S(2)}) collective-permute-start(bf16[4,32,256]{2,1,0:T(8,128)(2,1)S(1)} %get-tuple-element.38.refs_0_), channel_id=1, source_target_pairs={{0,2},{1,3},{2,0},{3,1},{4,6},{5,7},{6,4},{7,5},{8,10},{9,11},{10,... | collective-permute-start | bytes 196616 | tf_op jit(solution)/shard_map/ppermute | solution.py:37
  22.8 3.2 %collective-permute-done.8.refs_1_ = bf16[4,32,256]{2,1,0:T(8,128)(2,1)S(1)} collective-permute-done((bf16[4,32,256]{2,1,0:T(8,128)(2,1)S(1)}, bf16[4,32,256]{2,1,0:T(8,128)(2,1)S(1)}, u32[]{:S(2)}, u32[]{:S(2)}) %collective-permute-start.8) | collective-permute-done | bytes 65568 | tf_op jit(solution)/shard_map/ppermute | solution.py:37
  26.0 0.1 collective-permute-start.10
  26.1 2.1 %collective-permute-start.7 = (bf16[4,32,256]{2,1,0:T(8,128)(2,1)S(1)}, bf16[4,32,256]{2,1,0:T(8,128)(2,1)S(1)}, u32[]{:S(2)}, u32[]{:S(2)}) collective-permute-start(bf16[4,32,256]{2,1,0:T(8,128)(2,1)S(1)} %get-tuple-element.38.refs_0_), channel_id=1, source_target_pairs={{0,1},{1,0},{2,5},{3,4},{4,3},{5,2},{6,9},{7,8},{8,7},{9,6},{10,13... | collective-permute-start | bytes 196616 | tf_op jit(solution)/shard_map/ppermute | solution.py:37
  28.3 0.5 %collective-permute-start.6 = (bf16[4,32,256]{2,1,0:T(8,128)(2,1)S(1)}, bf16[4,32,256]{2,1,0:T(8,128)(2,1)S(1)}, u32[]{:S(2)}, u32[]{:S(2)}) collective-permute-start(bf16[4,32,256]{2,1,0:T(8,128)(2,1)S(1)} %get-tuple-element.38.refs_0_), channel_id=1, source_target_pairs={{0,1},{1,0},{2,4},{3,5},{4,2},{5,3},{6,8},{7,9},{8,6},{9,7},{10,12... | collective-permute-start | bytes 196616 | tf_op jit(solution)/shard_map/ppermute | solution.py:37
  28.7 0.0 collective-permute-done.9.refs_2_
  28.7 0.0 collective-permute-done.10.refs_3_
  28.7 0.8 %shard_map.62.refs_2_ = f32[8,32,256]{2,1,0:T(8,128)S(1)} custom-call(bf16[4,32,256]{2,1,0:T(8,128)(2,1)S(1)} %get-tuple-element.38.refs_0_, bf16[4,32,256]{2,1,0:T(8,128)(2,1)S(1)} %collective-permute-done.8.refs_1_, bf16[4,32,256]{2,1,0:T(8,128)(2,1)S(1)} %collective-permute-done.9.refs_2_, bf16[4,32,256]{2,1,0:T(8,128)(2,1)S(1)} %collective-permute-done.10.refs_3_, ...), custom_call_target="tpu_custom_call" | custom-call | flops 603979776 | bytes 1048576 | tf_op jit(solution)/shard_map/pallas_call | solution.py:66
  29.5 2.2 %collective-permute-done.7.refs_1_ = bf16[4,32,256]{2,1,0:T(8,128)(2,1)S(1)} collective-permute-done((bf16[4,32,256]{2,1,0:T(8,128)(2,1)S(1)}, bf16[4,32,256]{2,1,0:T(8,128)(2,1)S(1)}, u32[]{:S(2)}, u32[]{:S(2)}) %collective-permute-start.7) | collective-permute-done | bytes 65568 | tf_op jit(solution)/shard_map/ppermute | solution.py:37
  31.8 1.4 %collective-permute-done.6.refs_0_ = bf16[4,32,256]{2,1,0:T(8,128)(2,1)S(1)} collective-permute-done((bf16[4,32,256]{2,1,0:T(8,128)(2,1)S(1)}, bf16[4,32,256]{2,1,0:T(8,128)(2,1)S(1)}, u32[]{:S(2)}, u32[]{:S(2)}) %collective-permute-start.6) | collective-permute-done | bytes 65568 | tf_op jit(solution)/shard_map/ppermute | solution.py:37
  33.1 0.7 %shard_map.63 = (f32[4,32,256]{2,1,0:T(8,128)S(1)}, bf16[4,32,256]{2,1,0:T(8,128)(2,1)S(1)}) custom-call(bf16[4,32,256]{2,1,0:T(8,128)(2,1)S(1)} %collective-permute-done.6.refs_0_, bf16[4,32,256]{2,1,0:T(8,128)(2,1)S(1)} %collective-permute-done.7.refs_1_, f32[8,32,256]{2,1,0:T(8,128)S(1)} %shard_map.62.refs_2_, bf16[3,3,3,256,256]{4,3,2,1,0:T(8,128)(2,1)S(1)} %copy-done.1, ...), custom_call_target="tpu_custom_call" | custom-call | flops 301989888 | bytes 1048576 | tf_op jit(solution)/shard_map/pallas_call | solution.py:66
  33.8 0.4 %collective-permute-start.11 = (bf16[4,32,256]{2,1,0:T(8,128)(2,1)S(1)}, bf16[4,32,256]{2,1,0:T(8,128)(2,1)S(1)}, u32[]{:S(2)}, u32[]{:S(2)}) collective-permute-start(bf16[4,32,256]{2,1,0:T(8,128)(2,1)S(1)} %get-tuple-element.40), channel_id=1, source_target_pairs={{0,1},{1,0},{2,3},{3,2},{4,5},{5,4},{6,7},{7,6},{8,9},{9,8},{10,11... | collective-permute-start | bytes 196616 | tf_op jit(solution)/shard_map/ppermute | solution.py:37
  34.2 3.9 %collective-permute-done.11.refs_3_ = bf16[4,32,256]{2,1,0:T(8,128)(2,1)S(1)} collective-permute-done((bf16[4,32,256]{2,1,0:T(8,128)(2,1)S(1)}, bf16[4,32,256]{2,1,0:T(8,128)(2,1)S(1)}, u32[]{:S(2)}, u32[]{:S(2)}) %collective-permute-start.11) | collective-permute-done | bytes 65568 | tf_op jit(solution)/shard_map/ppermute | solution.py:37
  38.1 0.9 %shard_map.64 = bf16[2,8,64,256]{3,2,1,0:T(8,128)(2,1)} custom-call(bf16[8,64,256]{2,1,0:T(8,128)(2,1)S(1)} %get-tuple-element.36.refs_0_, bf16[8,64,256]{2,1,0:T(8,128)(2,1)S(1)} %get-tuple-element.37.refs_1_, f32[4,32,256]{2,1,0:T(8,128)S(1)} %get-tuple-element.39.refs_2_, bf16[4,32,256]{2,1,0:T(8,128)(2,1)S(1)} %collective-permute-done.11.refs_3_), custom_call_target="tpu_custom_call" | custom-call | flops 262144 | bytes 1048576 | tf_op jit(solution)/shard_map/pallas_call | solution.py:66
  (12 shorter events, 0.1 us)
Async XLA Ops:
  0.0 1.0 %copy-start.4 = (bf16[2,8,64,256]{3,2,1,0:T(8,128)(2,1)S(1)}, bf16[2,8,64,256]{3,2,1,0:T(8,128)(2,1)}, u32[]{:S(2)}) copy-start(bf16[2,8,64,256]{3,2,1,0:T(8,128)(2,1)} %refs_0_.1) | copy-start | bytes 1572868
  0.0 7.9 %collective-permute-start.4 = (bf16[2,8,64,256]{3,2,1,0:T(8,128)(2,1)}, bf16[2,8,64,256]{3,2,1,0:T(8,128)(2,1)S(1)}, u32[]{:S(2)}, u32[]{:S(2)}) collective-permute-start(bf16[2,8,64,256]{3,2,1,0:T(8,128)(2,1)} %refs_0_.1), channel_id=1, source_target_pairs={{0,2},{1,3},{2,0},{3,1},{4,6},{5,7},{6,4},{7,5},{8,10},{9,11},{10,... | collective-permute-start | bytes 1572872 | tf_op jit(solution)/shard_map/ppermute | solution.py:37
  1.0 6.9 %copy-start = (bf16[3,3,3,256,256]{4,3,2,1,0:T(8,128)(2,1)S(1)}, bf16[3,3,3,256,256]{4,3,2,1,0:T(8,128)(2,1)}, u32[]{:S(2)}) copy-start(bf16[3,3,3,256,256]{4,3,2,1,0:T(8,128)(2,1)} %refs_7_.3) | copy-start | bytes 10616836
  1.1 5.3 %collective-permute-start.2 = (bf16[2,2,64,256]{3,2,1,0:T(8,128)(2,1)S(1)}, bf16[2,2,64,256]{3,2,1,0:T(8,128)(2,1)S(1)}, u32[]{:S(2)}, u32[]{:S(2)}) collective-permute-start(bf16[2,2,64,256]{3,2,1,0:T(8,128)(2,1)S(1)} %get-tuple-element.25), channel_id=1, source_target_pairs={{0,1},{1,0},{2,3},{3,2},{4,5},{5,4},{6,7},{7,6},{8,9},{9,8},{10,11... | collective-permute-start | bytes 393224 | tf_op jit(solution)/shard_map/ppermute | solution.py:37
  1.7 14.7 %collective-permute-start = (bf16[8,64,256]{2,1,0:T(8,128)(2,1)S(1)}, bf16[8,64,256]{2,1,0:T(8,128)(2,1)S(1)}, u32[]{:S(2)}, u32[]{:S(2)}) collective-permute-start(bf16[8,64,256]{2,1,0:T(8,128)(2,1)S(1)} %get-tuple-element.23), channel_id=1, source_target_pairs={{0,1},{1,0},{2,4},{3,5},{4,2},{5,3},{6,8},{7,9},{8,6},{9,7},{10,12... | collective-permute-start | bytes 786440 | tf_op jit(solution)/shard_map/ppermute | solution.py:37
  2.3 10.7 %copy-start.2 = (bf16[3,3,3,256,256]{4,3,2,1,0:T(8,128)(2,1)S(1)}, bf16[3,3,3,256,256]{4,3,2,1,0:T(8,128)(2,1)}, u32[]{:S(2)}) copy-start(bf16[3,3,3,256,256]{4,3,2,1,0:T(8,128)(2,1)} %refs_8_.1) | copy-start | bytes 10616836
  2.3 15.4 %collective-permute-start.1 = (bf16[8,64,256]{2,1,0:T(8,128)(2,1)S(1)}, bf16[8,64,256]{2,1,0:T(8,128)(2,1)S(1)}, u32[]{:S(2)}, u32[]{:S(2)}) collective-permute-start(bf16[8,64,256]{2,1,0:T(8,128)(2,1)S(1)} %get-tuple-element.24), channel_id=1, source_target_pairs={{0,1},{1,0},{2,4},{3,5},{4,2},{5,3},{6,8},{7,9},{8,6},{9,7},{10,12... | collective-permute-start | bytes 786440 | tf_op jit(solution)/shard_map/ppermute | solution.py:37
  6.4 6.6 %collective-permute-start.5 = (bf16[2,2,64,256]{3,2,1,0:T(8,128)(2,1)S(1)}, bf16[2,2,64,256]{3,2,1,0:T(8,128)(2,1)S(1)}, u32[]{:S(2)}, u32[]{:S(2)}) collective-permute-start(bf16[2,2,64,256]{3,2,1,0:T(8,128)(2,1)S(1)} %collective-permute-done.2.refs_1_), channel_id=1, source_target_pairs={{0,2},{1,3},{2,0},{3,1},{4,6},{5,7},{6,4},{7,5},{8,10},{9,11},{10,... | collective-permute-start | bytes 393224 | tf_op jit(solution)/shard_map/ppermute | solution.py:37
  6.4 12.1 %collective-permute-start.3 = (bf16[2,2,64,256]{3,2,1,0:T(8,128)(2,1)S(1)}, bf16[2,2,64,256]{3,2,1,0:T(8,128)(2,1)S(1)}, u32[]{:S(2)}, u32[]{:S(2)}) collective-permute-start(bf16[2,2,64,256]{3,2,1,0:T(8,128)(2,1)S(1)} %collective-permute-done.2.refs_1_), channel_id=1, source_target_pairs={{0,1},{1,0},{2,4},{3,5},{4,2},{5,3},{6,8},{7,9},{8,6},{9,7},{10,12... | collective-permute-start | bytes 393224 | tf_op jit(solution)/shard_map/ppermute | solution.py:37
  18.5 10.3 %copy-start.1 = (bf16[3,3,3,256,256]{4,3,2,1,0:T(8,128)(2,1)S(1)}, bf16[3,3,3,256,256]{4,3,2,1,0:T(8,128)(2,1)}, u32[]{:S(2)}) copy-start(bf16[3,3,3,256,256]{4,3,2,1,0:T(8,128)(2,1)} %refs_3_.1) | copy-start | bytes 10616836
  21.2 11.9 %copy-start.3 = (bf16[256,256]{1,0:T(8,128)(2,1)S(1)}, bf16[256,256]{1,0:T(8,128)(2,1)}, u32[]{:S(2)}) copy-start(bf16[256,256]{1,0:T(8,128)(2,1)} %refs_4_.3) | copy-start | bytes 393220
  21.2 4.8 %collective-permute-start.8 = (bf16[4,32,256]{2,1,0:T(8,128)(2,1)S(1)}, bf16[4,32,256]{2,1,0:T(8,128)(2,1)S(1)}, u32[]{:S(2)}, u32[]{:S(2)}) collective-permute-start(bf16[4,32,256]{2,1,0:T(8,128)(2,1)S(1)} %get-tuple-element.38.refs_0_), channel_id=1, source_target_pairs={{0,1},{1,0},{2,3},{3,2},{4,5},{5,4},{6,7},{7,6},{8,9},{9,8},{10,11... | collective-permute-start | bytes 196616 | tf_op jit(solution)/shard_map/ppermute | solution.py:37
  21.8 6.9 %collective-permute-start.9 = (bf16[4,32,256]{2,1,0:T(8,128)(2,1)S(1)}, bf16[4,32,256]{2,1,0:T(8,128)(2,1)S(1)}, u32[]{:S(2)}, u32[]{:S(2)}) collective-permute-start(bf16[4,32,256]{2,1,0:T(8,128)(2,1)S(1)} %get-tuple-element.38.refs_0_), channel_id=1, source_target_pairs={{0,2},{1,3},{2,0},{3,1},{4,6},{5,7},{6,4},{7,5},{8,10},{9,11},{10,... | collective-permute-start | bytes 196616 | tf_op jit(solution)/shard_map/ppermute | solution.py:37
  26.0 2.7 %collective-permute-start.10 = (bf16[4,32,256]{2,1,0:T(8,128)(2,1)S(1)}, bf16[4,32,256]{2,1,0:T(8,128)(2,1)S(1)}, u32[]{:S(2)}, u32[]{:S(2)}) collective-permute-start(bf16[4,32,256]{2,1,0:T(8,128)(2,1)S(1)} %collective-permute-done.8.refs_1_), channel_id=1, source_target_pairs={{0,2},{1,3},{2,0},{3,1},{4,6},{5,7},{6,4},{7,5},{8,10},{9,11},{10,... | collective-permute-start | bytes 196616 | tf_op jit(solution)/shard_map/ppermute | solution.py:37
  26.1 5.6 %collective-permute-start.7 = (bf16[4,32,256]{2,1,0:T(8,128)(2,1)S(1)}, bf16[4,32,256]{2,1,0:T(8,128)(2,1)S(1)}, u32[]{:S(2)}, u32[]{:S(2)}) collective-permute-start(bf16[4,32,256]{2,1,0:T(8,128)(2,1)S(1)} %get-tuple-element.38.refs_0_), channel_id=1, source_target_pairs={{0,1},{1,0},{2,5},{3,4},{4,3},{5,2},{6,9},{7,8},{8,7},{9,6},{10,13... | collective-permute-start | bytes 196616 | tf_op jit(solution)/shard_map/ppermute | solution.py:37
  28.3 4.9 %collective-permute-start.6 = (bf16[4,32,256]{2,1,0:T(8,128)(2,1)S(1)}, bf16[4,32,256]{2,1,0:T(8,128)(2,1)S(1)}, u32[]{:S(2)}, u32[]{:S(2)}) collective-permute-start(bf16[4,32,256]{2,1,0:T(8,128)(2,1)S(1)} %get-tuple-element.38.refs_0_), channel_id=1, source_target_pairs={{0,1},{1,0},{2,4},{3,5},{4,2},{5,3},{6,8},{7,9},{8,6},{9,7},{10,12... | collective-permute-start | bytes 196616 | tf_op jit(solution)/shard_map/ppermute | solution.py:37
  33.8 4.3 %collective-permute-start.11 = (bf16[4,32,256]{2,1,0:T(8,128)(2,1)S(1)}, bf16[4,32,256]{2,1,0:T(8,128)(2,1)S(1)}, u32[]{:S(2)}, u32[]{:S(2)}) collective-permute-start(bf16[4,32,256]{2,1,0:T(8,128)(2,1)S(1)} %get-tuple-element.40), channel_id=1, source_target_pairs={{0,1},{1,0},{2,3},{3,2},{4,5},{5,4},{6,7},{7,6},{8,9},{9,8},{10,11... | collective-permute-start | bytes 196616 | tf_op jit(solution)/shard_map/ppermute | solution.py:37

commit v4 on v3

--- a/solution.py
+++ b/solution.py
@@ -285,25 +285,22 @@
         part[pl.ds(row, lines)] = conv_lines([(field, 0, tap(1, odd)), (field, 1, tap(2, odd))], row, lines, weight)
 
 
-def kernel_c2(*refs, chans):
-    part, weight, projection, own_part = refs[chans : chans + 4]
-    sent = refs[chans + 4 : 2 * chans + 3]
-    field, parts = refs[2 * chans + 3 :]
-    odd = lax.rem(lax.axis_index("brick"), 2)
-    chan = lax.axis_index("chan")
+def kernel_c2(*refs, chans, steps):
+    part, weight, projection = refs[chans : chans + 3]
+    results, field = refs[chans + 3 : -1], refs[-1]
+    odd = lax.rem(lax.axis_index("brick"), 2)
     total, depth = part.shape[0], part.shape[1]
     rows = total // chans
     fill_pooled(field, (refs[:chans],), has_far())
-    lines = tile_of(total)
-    for row in range(0, total, lines):
-        value = conv_lines([(field, 0, tap(0, odd))], row, lines, weight) + part[pl.ds(row, lines)]
-        value = jnp.maximum(value, 0.0).astype(BF16).reshape(lines * depth, weight.shape[4])
-        lifted = jnp.dot(value, projection[...], preferred_element_type=F32)
-        parts[pl.ds(row, lines)] = lifted.reshape(lines, depth, lifted.shape[1])
-    own_part[...] = parts[pl.ds(chan * rows, rows)]
-    for step in range(1, chans):
-        target = lax.rem(chan + step, chans)
-        sent[step - 1][...] = parts[pl.ds(target * rows, rows)].astype(BF16)
+    lines = tile_of(rows)
+    for step, result in zip(steps, results):
+        start = lax.rem(lax.axis_index("chan") + step, chans) * rows
+        for row in range(0, rows, lines):
+            value = conv_lines([(field, 0, tap(0, odd))], start + row, lines, weight)
+            value = jnp.maximum(value + part[pl.ds(start + row, lines)], 0.0).astype(BF16)
+            value = value.reshape(lines * depth, weight.shape[4])
+            lifted = jnp.dot(value, projection[...], preferred_element_type=F32)
+            result[pl.ds(row, lines)] = lifted.reshape(lines, depth, lifted.shape[1]).astype(result.dtype)
 
 
 def kernel_d(*refs):
@@ -418,18 +415,24 @@
         2 * plane_flops,
         12,
     )[0]
-    parts = call(
-        functools.partial(kernel_c2, chans=chans),
-        [*far_blocks, coarse_part, coarse_weight, projection],
-        [(part_shape, F32)] + [(part_shape, BF16)] * (chans - 1),
-        [pltpu.VMEM((1,) + coarse_field, BF16), pltpu.VMEM((coarse_rows, depth // 2, channels), F32)],
-        plane_flops,
-        12,
-    )
-    received = [exchange(part, "own", turn) for part, turn in zip(parts[1:], turns[1:])]
+    def last_part(steps, dtype):
+        return call(
+            functools.partial(kernel_c2, chans=chans, steps=steps),
+            [*far_blocks, coarse_part, coarse_weight, projection],
+            [(part_shape, dtype)] * len(steps),
+            [pltpu.VMEM((1,) + coarse_field, BF16)],
+            plane_flops * len(steps) // chans,
+            12,
+        )
+
+    received = []
+    if chans > 1:
+        sent = last_part(tuple(range(1, chans)), BF16)
+        received = [exchange(part, "own", turn) for part, turn in zip(sent, turns[1:])]
+    own_part = last_part((0,), F32)[0]
     return call(
         kernel_d,
-        [skipped_two, skipped_three, parts[0], *received],
+        [skipped_two, skipped_three, own_part, *received],
         [(volume.shape, BF16)],
         [pltpu.VMEM((channels // LANES, size_y // 2, depth, LANES), F32)],
         volume.size,

time: 39.2 us -> 39 us (level)
  waiting for transfers between devices: 12.8 us -> 12.3 us
    ppermute x12, waiting for transfers between devices: 12.8 us -> 12.3 us  [exchange(): return lax.ppermute(value, AXES, pairs)]
    pallas_call x10 -> x11, Pallas kernels: 15.6 us -> 15.9 us  [call(): pl.pallas_call(kernel, out_shape=out_shape, in_specs=[VMEM_SPEC] * len(in...]
  transfers between devices with their start and end apart: 12 -> 12, of which waited for: 5 -> 5; matrix products, arithmetic and copies ran while one was open for 0% -> 0% of each run, Pallas kernels for 29% -> 30%
where the time goes in v4:
time: 39 us; the launch traced here: 38.8 us
  Pallas kernels  15.9 us (41%)
  waiting for transfers between devices  12.3 us (32%)
  starting transfers between devices  9.46 us (24%)
  local copies, waits for them, and re-layouts  1.05 us (3%)
    pallas_call x11, Pallas kernels, call(): pl.pallas_call(kernel, out_shape=out_shape, in_specs=[VMEM_SPEC] * len(in...  15.9 us
    ppermute x12, waiting for transfers between devices, exchange(): return lax.ppermute(value, AXES, pairs)  12.3 us
    ppermute x12, starting transfers between devices, exchange(): return lax.ppermute(value, AXES, pairs)  9.46 us
    unnamed x10, local copies, waits for them, and re-layouts  1.05 us
  transfers between devices with their start and end apart: 12, of which 5 were waited for; matrix products, arithmetic and copies ran while one was open for 0% of the time, Pallas kernels for 30%

profile of v4, /device:TPU:26, one launch (start us, length us, event | category | flops | bytes accessed | tf_op | source)
XLA Modules:
  0.0 38.8 jit_solution(5699483525177004734)
XLA Ops:
  0.0 0.0 collective-permute-start.4
  0.0 1.0 %copy-done.4 = bf16[2,8,64,256]{3,2,1,0:T(8,128)(2,1)S(1)} copy-done((bf16[2,8,64,256]{3,2,1,0:T(8,128)(2,1)S(1)}, bf16[2,8,64,256]{3,2,1,0:T(8,128)(2,1)}, u32[]{:S(2)}) %copy-start.4) | copy-done | bytes 524312
  1.1 0.6 %collective-permute-start.2 = (bf16[2,2,64,256]{3,2,1,0:T(8,128)(2,1)S(1)}, bf16[2,2,64,256]{3,2,1,0:T(8,128)(2,1)S(1)}, u32[]{:S(2)}, u32[]{:S(2)}) collective-permute-start(bf16[2,2,64,256]{3,2,1,0:T(8,128)(2,1)S(1)} %get-tuple-element.23), channel_id=1, source_target_pairs={{0,1},{1,0},{2,3},{3,2},{4,5},{5,4},{6,7},{7,6},{8,9},{9,8},{10,11... | collective-permute-start | bytes 393224 | tf_op jit(solution)/shard_map/ppermute | solution.py:37
  1.7 0.6 %collective-permute-start = (bf16[8,64,256]{2,1,0:T(8,128)(2,1)S(1)}, bf16[8,64,256]{2,1,0:T(8,128)(2,1)S(1)}, u32[]{:S(2)}, u32[]{:S(2)}) collective-permute-start(bf16[8,64,256]{2,1,0:T(8,128)(2,1)S(1)} %get-tuple-element.21), channel_id=1, source_target_pairs={{0,1},{1,0},{2,4},{3,5},{4,2},{5,3},{6,8},{7,9},{8,6},{9,7},{10,12... | collective-permute-start | bytes 786440 | tf_op jit(solution)/shard_map/ppermute | solution.py:37
  2.3 2.1 %collective-permute-start.1 = (bf16[8,64,256]{2,1,0:T(8,128)(2,1)S(1)}, bf16[8,64,256]{2,1,0:T(8,128)(2,1)S(1)}, u32[]{:S(2)}, u32[]{:S(2)}) collective-permute-start(bf16[8,64,256]{2,1,0:T(8,128)(2,1)S(1)} %get-tuple-element.22), channel_id=1, source_target_pairs={{0,1},{1,0},{2,4},{3,5},{4,2},{5,3},{6,8},{7,9},{8,6},{9,7},{10,12... | collective-permute-start | bytes 786440 | tf_op jit(solution)/shard_map/ppermute | solution.py:37
  4.3 2.1 %collective-permute-done.2.refs_1_ = bf16[2,2,64,256]{3,2,1,0:T(8,128)(2,1)S(1)} collective-permute-done((bf16[2,2,64,256]{3,2,1,0:T(8,128)(2,1)S(1)}, bf16[2,2,64,256]{3,2,1,0:T(8,128)(2,1)S(1)}, u32[]{:S(2)}, u32[]{:S(2)}) %collective-permute-start.2) | collective-permute-done | bytes 131104 | tf_op jit(solution)/shard_map/ppermute | solution.py:37
  6.4 1.5 %collective-permute-start.3 = (bf16[2,2,64,256]{3,2,1,0:T(8,128)(2,1)S(1)}, bf16[2,2,64,256]{3,2,1,0:T(8,128)(2,1)S(1)}, u32[]{:S(2)}, u32[]{:S(2)}) collective-permute-start(bf16[2,2,64,256]{3,2,1,0:T(8,128)(2,1)S(1)} %collective-permute-done.2.refs_1_), channel_id=1, source_target_pairs={{0,1},{1,0},{2,4},{3,5},{4,2},{5,3},{6,8},{7,9},{8,6},{9,7},{10,12... | collective-permute-start | bytes 393224 | tf_op jit(solution)/shard_map/ppermute | solution.py:37
  7.9 0.0 collective-permute-done.4.near.refs_2_
  7.9 5.0 %shard_map.57 = (bf16[7,64,256]{2,1,0:T(8,128)(2,1)S(1)}, bf16[7,64,256]{2,1,0:T(8,128)(2,1)S(1)}, f32[7,64,256]{2,1,0:T(8,128)S(1)}, f32[7,64,256]{2,1,0:T(8,128)S(1)}) custom-call(bf16[2,8,64,256]{3,2,1,0:T(8,128)(2,1)S(1)} %copy-done.4, bf16[2,8,64,256]{3,2,1,0:T(8,128)(2,1)S(1)} %collective-permute-done.4.near.refs_2_, ...), custom_call_target="tpu_custom_call" | custom-call | flops 4756340736 | bytes 1048576 | tf_op jit(solution)/shard_map/pallas_call | solution.py:66
  13.0 0.0 collective-permute-done.5.refs_3_
  13.0 3.4 %shard_map.60 = (f32[8,64,256]{2,1,0:T(8,128)S(1)}, f32[8,64,256]{2,1,0:T(8,128)S(1)}, f32[2,64,256]{2,1,0:T(8,128)S(1)}, f32[2,64,256]{2,1,0:T(8,128)S(1)}) custom-call(bf16[2,8,64,256]{3,2,1,0:T(8,128)(2,1)S(1)} %copy-done.4, bf16[2,2,64,256]{3,2,1,0:T(8,128)(2,1)S(1)} %collective-permute-done.2.refs_1_, ...), custom_call_target="tpu_custom_call" | custom-call | flops 3170893824 | bytes 1048576 | tf_op jit(solution)/shard_map/pallas_call | solution.py:66
  16.4 1.3 %shard_map.58 = (f32[7,64,256]{2,1,0:T(8,128)S(1)}, bf16[7,64,256]{2,1,0:T(8,128)(2,1)S(1)}) custom-call(bf16[8,64,256]{2,1,0:T(8,128)(2,1)S(1)} %collective-permute-done.plane_one.refs_0_, f32[7,64,256]{2,1,0:T(8,128)S(1)} %get-tuple-element.24.part_one, f32[7,64,256]{2,1,0:T(8,128)S(1)} %get-tuple-element.25.part_two, bf16[3,3,3,256,256]{4,3,2,1,0:T(8,128)(2,1)S(1)} %copy-done), custom_call_target="tpu_custom_call" | custom-call | flops 1056964608 | bytes 1048576 | tf_op jit(solution)/shard_map/pallas_call | solution.py:66
  17.7 0.7 %shard_map.59.refs_3_ = bf16[7,64,256]{2,1,0:T(8,128)(2,1)S(1)} custom-call(bf16[8,64,256]{2,1,0:T(8,128)(2,1)S(1)} %collective-permute-done.1.plane_zero.refs_1_, f32[7,64,256]{2,1,0:T(8,128)S(1)} %get-tuple-element.26.part_one, bf16[3,3,3,256,256]{4,3,2,1,0:T(8,128)(2,1)S(1)} %copy-done), custom_call_target="tpu_custom_call" | custom-call | flops 528482304 | bytes 1048576 | tf_op jit(solution)/shard_map/pallas_call | solution.py:66
  18.5 0.0 copy-start.1
  18.5 2.8 %shard_map.61 = (bf16[8,64,256]{2,1,0:T(8,128)(2,1)S(1)}, bf16[8,64,256]{2,1,0:T(8,128)(2,1)S(1)}, bf16[4,32,256]{2,1,0:T(8,128)(2,1)S(1)}) custom-call(bf16[8,64,256]{2,1,0:T(8,128)(2,1)S(1)} %collective-permute-done.plane_one.refs_0_, bf16[8,64,256]{2,1,0:T(8,128)(2,1)S(1)} %collective-permute-done.1.plane_zero.refs_1_, ...), custom_call_target="tpu_custom_call" | custom-call | flops 2264924160 | bytes 1048576 | tf_op jit(solution)/shard_map/pallas_call | solution.py:66
  21.2 0.0 copy-start.3
  21.2 0.6 %collective-permute-start.8 = (bf16[4,32,256]{2,1,0:T(8,128)(2,1)S(1)}, bf16[4,32,256]{2,1,0:T(8,128)(2,1)S(1)}, u32[]{:S(2)}, u32[]{:S(2)}) collective-permute-start(bf16[4,32,256]{2,1,0:T(8,128)(2,1)S(1)} %get-tuple-element.36.refs_0_), channel_id=1, source_target_pairs={{0,1},{1,0},{2,3},{3,2},{4,5},{5,4},{6,7},{7,6},{8,9},{9,8},{10,11... | collective-permute-start | bytes 196616 | tf_op jit(solution)/shard_map/ppermute | solution.py:37
  21.8 1.0 %collective-permute-start.9 = (bf16[4,32,256]{2,1,0:T(8,128)(2,1)S(1)}, bf16[4,32,256]{2,1,0:T(8,128)(2,1)S(1)}, u32[]{:S(2)}, u32[]{:S(2)}) collective-permute-start(bf16[4,32,256]{2,1,0:T(8,128)(2,1)S(1)} %get-tuple-element.36.refs_0_), channel_id=1, source_target_pairs={{0,2},{1,3},{2,0},{3,1},{4,6},{5,7},{6,4},{7,5},{8,10},{9,11},{10,... | collective-permute-start | bytes 196616 | tf_op jit(solution)/shard_map/ppermute | solution.py:37
  22.8 3.2 %collective-permute-done.8.refs_1_ = bf16[4,32,256]{2,1,0:T(8,128)(2,1)S(1)} collective-permute-done((bf16[4,32,256]{2,1,0:T(8,128)(2,1)S(1)}, bf16[4,32,256]{2,1,0:T(8,128)(2,1)S(1)}, u32[]{:S(2)}, u32[]{:S(2)}) %collective-permute-start.8) | collective-permute-done | bytes 65568 | tf_op jit(solution)/shard_map/ppermute | solution.py:37
  26.0 0.1 collective-permute-start.10
  26.1 2.1 %collective-permute-start.7 = (bf16[4,32,256]{2,1,0:T(8,128)(2,1)S(1)}, bf16[4,32,256]{2,1,0:T(8,128)(2,1)S(1)}, u32[]{:S(2)}, u32[]{:S(2)}) collective-permute-start(bf16[4,32,256]{2,1,0:T(8,128)(2,1)S(1)} %get-tuple-element.36.refs_0_), channel_id=1, source_target_pairs={{0,1},{1,0},{2,5},{3,4},{4,3},{5,2},{6,9},{7,8},{8,7},{9,6},{10,13... | collective-permute-start | bytes 196616 | tf_op jit(solution)/shard_map/ppermute | solution.py:37
  28.3 0.5 %collective-permute-start.6 = (bf16[4,32,256]{2,1,0:T(8,128)(2,1)S(1)}, bf16[4,32,256]{2,1,0:T(8,128)(2,1)S(1)}, u32[]{:S(2)}, u32[]{:S(2)}) collective-permute-start(bf16[4,32,256]{2,1,0:T(8,128)(2,1)S(1)} %get-tuple-element.36.refs_0_), channel_id=1, source_target_pairs={{0,1},{1,0},{2,4},{3,5},{4,2},{5,3},{6,8},{7,9},{8,6},{9,7},{10,12... | collective-permute-start | bytes 196616 | tf_op jit(solution)/shard_map/ppermute | solution.py:37
  28.7 0.0 collective-permute-done.9.refs_2_
  28.7 0.0 collective-permute-done.10.refs_3_
  28.7 0.8 %shard_map.62.refs_2_ = f32[8,32,256]{2,1,0:T(8,128)S(1)} custom-call(bf16[4,32,256]{2,1,0:T(8,128)(2,1)S(1)} %get-tuple-element.36.refs_0_, bf16[4,32,256]{2,1,0:T(8,128)(2,1)S(1)} %collective-permute-done.8.refs_1_, bf16[4,32,256]{2,1,0:T(8,128)(2,1)S(1)} %collective-permute-done.9.refs_2_, bf16[4,32,256]{2,1,0:T(8,128)(2,1)S(1)} %collective-permute-done.10.refs_3_, ...), custom_call_target="tpu_custom_call" | custom-call | flops 603979776 | bytes 1048576 | tf_op jit(solution)/shard_map/pallas_call | solution.py:66
  29.5 2.2 %collective-permute-done.7.refs_1_ = bf16[4,32,256]{2,1,0:T(8,128)(2,1)S(1)} collective-permute-done((bf16[4,32,256]{2,1,0:T(8,128)(2,1)S(1)}, bf16[4,32,256]{2,1,0:T(8,128)(2,1)S(1)}, u32[]{:S(2)}, u32[]{:S(2)}) %collective-permute-start.7) | collective-permute-done | bytes 65568 | tf_op jit(solution)/shard_map/ppermute | solution.py:37
  31.8 1.4 %collective-permute-done.6.refs_0_ = bf16[4,32,256]{2,1,0:T(8,128)(2,1)S(1)} collective-permute-done((bf16[4,32,256]{2,1,0:T(8,128)(2,1)S(1)}, bf16[4,32,256]{2,1,0:T(8,128)(2,1)S(1)}, u32[]{:S(2)}, u32[]{:S(2)}) %collective-permute-start.6) | collective-permute-done | bytes 65568 | tf_op jit(solution)/shard_map/ppermute | solution.py:37
  33.1 0.5 %shard_map.64 = bf16[4,32,256]{2,1,0:T(8,128)(2,1)S(1)} custom-call(bf16[4,32,256]{2,1,0:T(8,128)(2,1)S(1)} %collective-permute-done.6.refs_0_, bf16[4,32,256]{2,1,0:T(8,128)(2,1)S(1)} %collective-permute-done.7.refs_1_, f32[8,32,256]{2,1,0:T(8,128)S(1)} %shard_map.62.refs_2_, bf16[3,3,3,256,256]{4,3,2,1,0:T(8,128)(2,1)S(1)} %copy-done.1, ...), custom_call_target="tpu_custom_call" | custom-call | flops 150994944 | bytes 1048576 | tf_op jit(solution)/shard_map/pallas_call | solution.py:66
  33.6 0.4 %collective-permute-start.11 = (bf16[4,32,256]{2,1,0:T(8,128)(2,1)S(1)}, bf16[4,32,256]{2,1,0:T(8,128)(2,1)S(1)}, u32[]{:S(2)}, u32[]{:S(2)}) collective-permute-start(bf16[4,32,256]{2,1,0:T(8,128)(2,1)S(1)} %shard_map.64), channel_id=1, source_target_pairs={{0,1},{1,0},{2,3},{3,2},{4,5},{5,4},{6,7},{7,6},{8,9},{9,8},{10,11... | collective-permute-start | bytes 196616 | tf_op jit(solution)/shard_map/ppermute | solution.py:37
  34.0 0.5 %shard_map.63.refs_2_ = f32[4,32,256]{2,1,0:T(8,128)S(1)} custom-call(bf16[4,32,256]{2,1,0:T(8,128)(2,1)S(1)} %collective-permute-done.6.refs_0_, bf16[4,32,256]{2,1,0:T(8,128)(2,1)S(1)} %collective-permute-done.7.refs_1_, f32[8,32,256]{2,1,0:T(8,128)S(1)} %shard_map.62.refs_2_, bf16[3,3,3,256,256]{4,3,2,1,0:T(8,128)(2,1)S(1)} %copy-done.1, ...), custom_call_target="tpu_custom_call" | custom-call | flops 150994944 | bytes 1048576 | tf_op jit(solution)/shard_map/pallas_call | solution.py:66
  34.5 3.5 %collective-permute-done.11.refs_3_ = bf16[4,32,256]{2,1,0:T(8,128)(2,1)S(1)} collective-permute-done((bf16[4,32,256]{2,1,0:T(8,128)(2,1)S(1)}, bf16[4,32,256]{2,1,0:T(8,128)(2,1)S(1)}, u32[]{:S(2)}, u32[]{:S(2)}) %collective-permute-start.11) | collective-permute-done | bytes 65568 | tf_op jit(solution)/shard_map/ppermute | solution.py:37
  37.9 0.9 %shard_map.65 = bf16[2,8,64,256]{3,2,1,0:T(8,128)(2,1)} custom-call(bf16[8,64,256]{2,1,0:T(8,128)(2,1)S(1)} %get-tuple-element.34.refs_0_, bf16[8,64,256]{2,1,0:T(8,128)(2,1)S(1)} %get-tuple-element.35.refs_1_, f32[4,32,256]{2,1,0:T(8,128)S(1)} %shard_map.63.refs_2_, bf16[4,32,256]{2,1,0:T(8,128)(2,1)S(1)} %collective-permute-done.11.refs_3_), custom_call_target="tpu_custom_call" | custom-call | flops 262144 | bytes 1048576 | tf_op jit(solution)/shard_map/pallas_call | solution.py:66
  (13 shorter events, 0.1 us)
Async XLA Ops:
  0.0 1.0 %copy-start.4 = (bf16[2,8,64,256]{3,2,1,0:T(8,128)(2,1)S(1)}, bf16[2,8,64,256]{3,2,1,0:T(8,128)(2,1)}, u32[]{:S(2)}) copy-start(bf16[2,8,64,256]{3,2,1,0:T(8,128)(2,1)} %refs_0_.1) | copy-start | bytes 1572868
  0.0 7.9 %collective-permute-start.4 = (bf16[2,8,64,256]{3,2,1,0:T(8,128)(2,1)}, bf16[2,8,64,256]{3,2,1,0:T(8,128)(2,1)S(1)}, u32[]{:S(2)}, u32[]{:S(2)}) collective-permute-start(bf16[2,8,64,256]{3,2,1,0:T(8,128)(2,1)} %refs_0_.1), channel_id=1, source_target_pairs={{0,2},{1,3},{2,0},{3,1},{4,6},{5,7},{6,4},{7,5},{8,10},{9,11},{10,... | collective-permute-start | bytes 1572872 | tf_op jit(solution)/shard_map/ppermute | solution.py:37
  1.0 6.9 %copy-start = (bf16[3,3,3,256,256]{4,3,2,1,0:T(8,128)(2,1)S(1)}, bf16[3,3,3,256,256]{4,3,2,1,0:T(8,128)(2,1)}, u32[]{:S(2)}) copy-start(bf16[3,3,3,256,256]{4,3,2,1,0:T(8,128)(2,1)} %refs_7_.3) | copy-start | bytes 10616836
  1.1 5.3 %collective-permute-start.2 = (bf16[2,2,64,256]{3,2,1,0:T(8,128)(2,1)S(1)}, bf16[2,2,64,256]{3,2,1,0:T(8,128)(2,1)S(1)}, u32[]{:S(2)}, u32[]{:S(2)}) collective-permute-start(bf16[2,2,64,256]{3,2,1,0:T(8,128)(2,1)S(1)} %get-tuple-element.23), channel_id=1, source_target_pairs={{0,1},{1,0},{2,3},{3,2},{4,5},{5,4},{6,7},{7,6},{8,9},{9,8},{10,11... | collective-permute-start | bytes 393224 | tf_op jit(solution)/shard_map/ppermute | solution.py:37
  1.7 14.7 %collective-permute-start = (bf16[8,64,256]{2,1,0:T(8,128)(2,1)S(1)}, bf16[8,64,256]{2,1,0:T(8,128)(2,1)S(1)}, u32[]{:S(2)}, u32[]{:S(2)}) collective-permute-start(bf16[8,64,256]{2,1,0:T(8,128)(2,1)S(1)} %get-tuple-element.21), channel_id=1, source_target_pairs={{0,1},{1,0},{2,4},{3,5},{4,2},{5,3},{6,8},{7,9},{8,6},{9,7},{10,12... | collective-permute-start | bytes 786440 | tf_op jit(solution)/shard_map/ppermute | solution.py:37
  2.3 10.7 %copy-start.2 = (bf16[3,3,3,256,256]{4,3,2,1,0:T(8,128)(2,1)S(1)}, bf16[3,3,3,256,256]{4,3,2,1,0:T(8,128)(2,1)}, u32[]{:S(2)}) copy-start(bf16[3,3,3,256,256]{4,3,2,1,0:T(8,128)(2,1)} %refs_8_.1) | copy-start | bytes 10616836
  2.3 15.4 %collective-permute-start.1 = (bf16[8,64,256]{2,1,0:T(8,128)(2,1)S(1)}, bf16[8,64,256]{2,1,0:T(8,128)(2,1)S(1)}, u32[]{:S(2)}, u32[]{:S(2)}) collective-permute-start(bf16[8,64,256]{2,1,0:T(8,128)(2,1)S(1)} %get-tuple-element.22), channel_id=1, source_target_pairs={{0,1},{1,0},{2,4},{3,5},{4,2},{5,3},{6,8},{7,9},{8,6},{9,7},{10,12... | collective-permute-start | bytes 786440 | tf_op jit(solution)/shard_map/ppermute | solution.py:37
  6.4 6.6 %collective-permute-start.5 = (bf16[2,2,64,256]{3,2,1,0:T(8,128)(2,1)S(1)}, bf16[2,2,64,256]{3,2,1,0:T(8,128)(2,1)S(1)}, u32[]{:S(2)}, u32[]{:S(2)}) collective-permute-start(bf16[2,2,64,256]{3,2,1,0:T(8,128)(2,1)S(1)} %collective-permute-done.2.refs_1_), channel_id=1, source_target_pairs={{0,2},{1,3},{2,0},{3,1},{4,6},{5,7},{6,4},{7,5},{8,10},{9,11},{10,... | collective-permute-start | bytes 393224 | tf_op jit(solution)/shard_map/ppermute | solution.py:37
  6.4 12.1 %collective-permute-start.3 = (bf16[2,2,64,256]{3,2,1,0:T(8,128)(2,1)S(1)}, bf16[2,2,64,256]{3,2,1,0:T(8,128)(2,1)S(1)}, u32[]{:S(2)}, u32[]{:S(2)}) collective-permute-start(bf16[2,2,64,256]{3,2,1,0:T(8,128)(2,1)S(1)} %collective-permute-done.2.refs_1_), channel_id=1, source_target_pairs={{0,1},{1,0},{2,4},{3,5},{4,2},{5,3},{6,8},{7,9},{8,6},{9,7},{10,12... | collective-permute-start | bytes 393224 | tf_op jit(solution)/shard_map/ppermute | solution.py:37
  18.5 10.3 %copy-start.1 = (bf16[3,3,3,256,256]{4,3,2,1,0:T(8,128)(2,1)S(1)}, bf16[3,3,3,256,256]{4,3,2,1,0:T(8,128)(2,1)}, u32[]{:S(2)}) copy-start(bf16[3,3,3,256,256]{4,3,2,1,0:T(8,128)(2,1)} %refs_3_.3) | copy-start | bytes 10616836
  21.2 11.9 %copy-start.3 = (bf16[256,256]{1,0:T(8,128)(2,1)S(1)}, bf16[256,256]{1,0:T(8,128)(2,1)}, u32[]{:S(2)}) copy-start(bf16[256,256]{1,0:T(8,128)(2,1)} %refs_4_.5) | copy-start | bytes 393220
  21.2 4.8 %collective-permute-start.8 = (bf16[4,32,256]{2,1,0:T(8,128)(2,1)S(1)}, bf16[4,32,256]{2,1,0:T(8,128)(2,1)S(1)}, u32[]{:S(2)}, u32[]{:S(2)}) collective-permute-start(bf16[4,32,256]{2,1,0:T(8,128)(2,1)S(1)} %get-tuple-element.36.refs_0_), channel_id=1, source_target_pairs={{0,1},{1,0},{2,3},{3,2},{4,5},{5,4},{6,7},{7,6},{8,9},{9,8},{10,11... | collective-permute-start | bytes 196616 | tf_op jit(solution)/shard_map/ppermute | solution.py:37
  21.8 6.9 %collective-permute-start.9 = (bf16[4,32,256]{2,1,0:T(8,128)(2,1)S(1)}, bf16[4,32,256]{2,1,0:T(8,128)(2,1)S(1)}, u32[]{:S(2)}, u32[]{:S(2)}) collective-permute-start(bf16[4,32,256]{2,1,0:T(8,128)(2,1)S(1)} %get-tuple-element.36.refs_0_), channel_id=1, source_target_pairs={{0,2},{1,3},{2,0},{3,1},{4,6},{5,7},{6,4},{7,5},{8,10},{9,11},{10,... | collective-permute-start | bytes 196616 | tf_op jit(solution)/shard_map/ppermute | solution.py:37
  26.0 2.7 %collective-permute-start.10 = (bf16[4,32,256]{2,1,0:T(8,128)(2,1)S(1)}, bf16[4,32,256]{2,1,0:T(8,128)(2,1)S(1)}, u32[]{:S(2)}, u32[]{:S(2)}) collective-permute-start(bf16[4,32,256]{2,1,0:T(8,128)(2,1)S(1)} %collective-permute-done.8.refs_1_), channel_id=1, source_target_pairs={{0,2},{1,3},{2,0},{3,1},{4,6},{5,7},{6,4},{7,5},{8,10},{9,11},{10,... | collective-permute-start | bytes 196616 | tf_op jit(solution)/shard_map/ppermute | solution.py:37
  26.1 5.6 %collective-permute-start.7 = (bf16[4,32,256]{2,1,0:T(8,128)(2,1)S(1)}, bf16[4,32,256]{2,1,0:T(8,128)(2,1)S(1)}, u32[]{:S(2)}, u32[]{:S(2)}) collective-permute-start(bf16[4,32,256]{2,1,0:T(8,128)(2,1)S(1)} %get-tuple-element.36.refs_0_), channel_id=1, source_target_pairs={{0,1},{1,0},{2,5},{3,4},{4,3},{5,2},{6,9},{7,8},{8,7},{9,6},{10,13... | collective-permute-start | bytes 196616 | tf_op jit(solution)/shard_map/ppermute | solution.py:37
  28.3 4.9 %collective-permute-start.6 = (bf16[4,32,256]{2,1,0:T(8,128)(2,1)S(1)}, bf16[4,32,256]{2,1,0:T(8,128)(2,1)S(1)}, u32[]{:S(2)}, u32[]{:S(2)}) collective-permute-start(bf16[4,32,256]{2,1,0:T(8,128)(2,1)S(1)} %get-tuple-element.36.refs_0_), channel_id=1, source_target_pairs={{0,1},{1,0},{2,4},{3,5},{4,2},{5,3},{6,8},{7,9},{8,6},{9,7},{10,12... | collective-permute-start | bytes 196616 | tf_op jit(solution)/shard_map/ppermute | solution.py:37
  33.6 4.3 %collective-permute-start.11 = (bf16[4,32,256]{2,1,0:T(8,128)(2,1)S(1)}, bf16[4,32,256]{2,1,0:T(8,128)(2,1)S(1)}, u32[]{:S(2)}, u32[]{:S(2)}) collective-permute-start(bf16[4,32,256]{2,1,0:T(8,128)(2,1)S(1)} %shard_map.64), channel_id=1, source_target_pairs={{0,1},{1,0},{2,3},{3,2},{4,5},{5,4},{6,7},{7,6},{8,9},{9,8},{10,11... | collective-permute-start | bytes 196616 | tf_op jit(solution)/shard_map/ppermute | solution.py:37
